TPU v7x, 32 devices: a whole 2x2x4 slice. The times are simulated.
32 devices in a mesh: angle: 4 (over z), pos: 8 (over y, x, core).
Axes of the slice: x: 2, y: 2, z: 4, core: 2. Of those that a mesh axis runs over, the one named last changes fastest.
Arguments:
- amplitude: float32 [4, 32, 128, 128], P('angle', 'pos'), may hold values from 0 to 2.5
- offsets: int32 [4, 32, 2], P('angle', 'pos'), may hold values from 0 to 896, as said below
- probe_field: float32 [2, 128, 128], replicated, may hold values from -5 to 5
- object_field: float32 [4, 2, 1024, 1024], P('angle', None, 'pos'), may hold values from -5 to 5
- interp_index: int32 [4, 2, 1024], replicated, may hold values from 0 to 1022
- interp_weight: float32 [4, 2, 1024], replicated, may hold values from 0 to 1
Outputs:
- new_object: float32 [4, 2, 1024, 1024], P('angle', None, 'pos')
- new_probe: float32 [2, 128, 128], replicated
- recon: float32 [8, 128, 2, 1024], P('pos', 'angle')
Inputs may be any that keep to these rules, and one draw needn't show every extreme that they name: For position j, offsets[a, j, 0] = max(0, min(896, (j // 4) * 128 - 128 // 2 + u)) with 0 <= u < 128; offsets[a, j, 1] lies in 0 to 896.
All inputs are finite; a program needn't handle non-finite values.
Results may differ from a plain program's by a relative error of at most 0.00007.
Values sent between devices are 32-bit elements; how exact they have to be, the bound alone decides.
No kernel may reach another device: no remote copies, remote signals or barrier semaphores. Data moves between devices by JAX's collectives and lax.ppermute only.
A program may use at most 64 MiB of HBM per device.

v0:
```python
import math

import jax
import jax.numpy as jnp
from jax import lax
from jax.sharding import PartitionSpec as P


def with_halo(block, sides, width):
    for axis, dim in sides:
        count = lax.axis_size(axis)
        forward = [(i, i + 1) for i in range(count - 1)]
        backward = [(target, source) for source, target in forward]
        low = lax.ppermute(
            lax.slice_in_dim(block, block.shape[dim] - width, None, axis=dim), axis, forward
        )
        high = lax.ppermute(lax.slice_in_dim(block, 0, width, axis=dim), axis, backward)
        block = jnp.concatenate([low, block, high], axis=dim)
    return block


def passed_along(array, axis, by):
    length = lax.axis_size(axis)
    pairs = [(i, i + by) for i in range(length) if 0 <= i + by < length]
    return lax.ppermute(array, axis, pairs)


def ramp_matrix(length):
    ramp = jnp.arange(length, dtype=jnp.int32)
    differ = ramp[:, None] - ramp[None, :]
    spread = differ.astype(jnp.float32)
    squared = jnp.maximum(spread * spread, 1.0)
    odd_terms = jnp.where(differ % 2 != 0, -1.0 / (math.pi * math.pi * squared), 0.0)
    return jnp.where(differ == 0, 0.25, odd_terms)


def dft_tables(length):
    ramp = jnp.arange(length, dtype=jnp.int32)
    phases = ramp[:, None] * ramp[None, :] % length
    theta = phases.astype(jnp.float32) * (2.0 * math.pi / length)
    factor = 1.0 / math.sqrt(length)
    return (jnp.cos(theta) * factor, -jnp.sin(theta) * factor)


def left_product(table_real, table_imag, value_real, value_imag):
    high = lax.Precision.HIGHEST
    first = jnp.einsum("ij,bjk->bik", table_real, value_real, precision=high)
    second = jnp.einsum("ij,bjk->bik", table_imag, value_imag, precision=high)
    third = jnp.einsum("ij,bjk->bik", table_real, value_imag, precision=high)
    fourth = jnp.einsum("ij,bjk->bik", table_imag, value_real, precision=high)
    return (first - second, third + fourth)


def right_product(value_real, value_imag, table_real, table_imag):
    high = lax.Precision.HIGHEST
    first = jnp.einsum("bij,jk->bik", value_real, table_real, precision=high)
    second = jnp.einsum("bij,jk->bik", value_imag, table_imag, precision=high)
    third = jnp.einsum("bij,jk->bik", value_imag, table_real, precision=high)
    fourth = jnp.einsum("bij,jk->bik", value_real, table_imag, precision=high)
    return (first - second, third + fourth)


def transform_both(value_real, value_imag, table_real, table_imag):
    middle_real, middle_imag = left_product(table_real, table_imag, value_real, value_imag)
    return right_product(middle_real, middle_imag, table_real, table_imag)


def on_device(amplitude, offsets, probe_field, object_field, interp_index, interp_weight):
    band = object_field.shape[2]
    width = object_field.shape[3]
    patch = probe_field.shape[1]
    half_patch = patch // 2
    per_device = offsets.shape[1]
    row_index = lax.axis_index("pos")
    extended = with_halo(object_field, (("pos", 2),), half_patch)
    anchor = row_index * band - half_patch
    local_rows = offsets[:, :, 0] - anchor
    columns = offsets[:, :, 1]
    table_real, table_imag = dft_tables(patch)
    probe_real = probe_field[0]
    probe_imag = probe_field[1]
    power = probe_real * probe_real + probe_imag * probe_imag
    channels = 3

    def one_angle(inputs):
        amps, rows, cols, layer = inputs

        def take_patch(first_row, first_col):
            return lax.dynamic_slice(layer, (jnp.int32(0), first_row, first_col), (2, patch, patch))

        cut = jax.vmap(take_patch)(rows, cols)
        patch_real = cut[:, 0]
        patch_imag = cut[:, 1]
        wave_real = probe_real * patch_real - probe_imag * patch_imag
        wave_imag = probe_real * patch_imag + probe_imag * patch_real
        spec_real, spec_imag = transform_both(wave_real, wave_imag, table_real, table_imag)
        magnitude = jnp.sqrt(spec_real * spec_real + spec_imag * spec_imag)
        factor = amps / jnp.maximum(magnitude, 0.5)
        back_real, back_imag = transform_both(
            factor * spec_real, factor * spec_imag, table_real, -table_imag
        )
        diff_real = back_real - wave_real
        diff_imag = back_imag - wave_imag
        grad_real = probe_real * diff_real + probe_imag * diff_imag
        grad_imag = probe_real * diff_imag - probe_imag * diff_real
        numer_real = jnp.sum(patch_real * diff_real + patch_imag * diff_imag, axis=0)
        numer_imag = jnp.sum(patch_real * diff_imag - patch_imag * diff_real, axis=0)
        denom = jnp.sum(patch_real * patch_real + patch_imag * patch_imag, axis=0)
        pieces = [grad_real, grad_imag]
        pieces.append(jnp.broadcast_to(power, grad_real.shape))
        stacked = jnp.stack(pieces, axis=1)

        def accumulate(count, total):
            start = (jnp.int32(0), rows[count], cols[count])
            current = lax.dynamic_slice(total, start, (channels, patch, patch))
            return lax.dynamic_update_slice(total, current + stacked[count], start)

        total = lax.fori_loop(
            0, per_device, accumulate, jnp.zeros((channels, band + patch, width), jnp.float32)
        )
        return (total, jnp.stack([numer_real, numer_imag]), denom)

    buffers, numers, denoms = lax.map(one_angle, (amplitude, local_rows, columns, extended))
    upper_rims = buffers[:, :, :half_patch]
    lower_rims = buffers[:, :, half_patch + band :]
    from_below = passed_along(upper_rims, "pos", -1)
    from_above = passed_along(lower_rims, "pos", 1)
    owned = buffers[:, :, half_patch : half_patch + band]
    owned = owned.at[:, :, :half_patch].add(from_above)
    owned = owned.at[:, :, band - half_patch :].add(from_below)
    weight_sum = owned[:, 2]
    new_object = object_field + owned[:, :2] / (weight_sum[:, None] + 1.0)
    numer_all, denom_all = lax.psum(
        (jnp.sum(numers, axis=0), jnp.sum(denoms, axis=0)), ("angle", "pos")
    )
    new_probe = probe_field + numer_all / (denom_all + 1.0)
    regrouped = lax.all_to_all(new_object[:, 1], "angle", split_axis=1, concat_axis=0, tiled=True)
    total_angles = regrouped.shape[0]
    slice_count = regrouped.shape[1]
    sinogram = jnp.transpose(regrouped, (1, 0, 2))
    filtered = jnp.dot(
        sinogram.reshape(slice_count * total_angles, width),
        ramp_matrix(width),
        precision=lax.Precision.HIGHEST,
    )
    filtered = jnp.moveaxis(filtered.reshape(slice_count, total_angles, width), 1, 0)
    zwin = interp_index.shape[1]
    bins = jnp.arange(width, dtype=jnp.int32)[:, None]

    def back_step(total, inputs):
        rows_angle, index_angle, weight_angle = inputs
        results = []
        for depth in range(zwin):
            lower_bin = index_angle[depth][None, :]
            upper_weight = weight_angle[depth][None, :]
            matrix = jnp.where(bins == lower_bin, 1.0 - upper_weight, 0.0) + jnp.where(
                bins == lower_bin + 1, upper_weight, 0.0
            )
            results.append(jnp.dot(rows_angle, matrix, precision=lax.Precision.HIGHEST))
        return (total + jnp.concatenate(results, axis=1), None)

    total, unused = lax.scan(
        back_step,
        jnp.zeros((slice_count, zwin * width), jnp.float32),
        (filtered, interp_index, interp_weight),
    )
    recon = (total * (math.pi / total_angles)).reshape(1, slice_count, zwin, width)
    return (new_object, new_probe, recon)


def solution(mesh):
    placed = (
        P("angle", "pos", None, None),
        P("angle", "pos", None),
        P(),
        P("angle", None, "pos", None),
        P(),
        P(),
    )
    return jax.shard_map(
        on_device,
        mesh=mesh,
        in_specs=placed,
        out_specs=(P("angle", None, "pos", None), P(), P("pos", "angle", None, None)),
        check_vma=False,
    )
```

profile of v0, /device:TPU:3, one launch (start us, length us, event | category | flops | bytes accessed | tf_op | source)
XLA Modules:
  0.0 305.6 jit_solution(7285216097695240660)
XLA Ops:
  7.2 1.4 fusion.203
  8.5 3.7 %collective-permute-start = (f32[1,2,64,1024]{3,2,1,0:T(8,128)S(1)}, f32[1,2,64,1024]{3,2,1,0:T(8,128)S(1)}, u32[]{:S(2)}, u32[]{:S(2)}) collective-permute-start(f32[1,2,64,1024]{3,2,1,0:T(8,128)S(1)} %get-tuple-element.327), channel_id=1, source_target_pairs={{0,1},{1,2},{2,3},{3,4},{4,5},{5,6},{6,7},{8,9},{9,10},{10,11},{11... | collective-permute-start | bytes 1572872 | tf_op jit(solution)/shard_map/ppermute | solution.py:14
  12.2 1.9 collective-permute-start.1
  15.8 0.9 multiply_add_fusion
  16.7 0.9 slice_bitcast_fusion.2
  17.6 3.6 %collective-permute-done = f32[1,2,64,1024]{3,2,1,0:T(8,128)S(1)} collective-permute-done((f32[1,2,64,1024]{3,2,1,0:T(8,128)S(1)}, f32[1,2,64,1024]{3,2,1,0:T(8,128)S(1)}, u32[]{:S(2)}, u32[]{:S(2)}) %collective-permute-start) | collective-permute-done | bytes 524320 | tf_op jit(solution)/shard_map/ppermute | solution.py:14
  22.0 3.7 %collective-permute-done.1 = f32[1,2,64,1024]{3,2,1,0:T(8,128)} collective-permute-done((f32[1,2,64,1024]{3,2,1,0:T(8,128)S(1)}, f32[1,2,64,1024]{3,2,1,0:T(8,128)}, u32[]{:S(2)}, u32[]{:S(2)}) %collective-permute-start.1) | collective-permute-done | bytes 524320 | tf_op jit(solution)/shard_map/ppermute | solution.py:17
  25.7 1.4 maximum_bitcast_fusion
  27.1 10.2 %while.38 = (s32[]{:T(128)}, f32[2,256,1024]{2,1,0:T(8,128)S(1)}, s32[4,3]{1,0:T(4,128)S(1)}, f32[4,2,128,128]{3,2,0,1:T(8,128)}, s32[]{:T(128)}) while((s32[]{:T(128)}, f32[2,256,1024]{2,1,0:T(8,128)S(1)}, s32[4,3]{1,0:T(4,128)S(1)}, f32[4,2,128,128]{3,2,0,1:T(8,128)}, s32[]{:T(128)}) %tuple.101), condition=%wide.while_cond.2, body=%wide.while_body.2.sunk | while | flops 2 | bytes 263785 | solution.py:89
  27.7 2.0 bitcast_dynamic-update-slice_fusion.2
  30.3 2.0 bitcast_dynamic-update-slice_fusion.2
  32.8 1.9 bitcast_dynamic-update-slice_fusion.2
  35.4 2.0 bitcast_dynamic-update-slice_fusion.2
  37.3 1.1 fusion.65
  49.9 1.6 fusion.67
  51.6 0.9 pad_maximum_fusion
  52.9 35.6 %while.37 = (s32[]{:T(128)}, f32[3,256,1024]{2,1,0:T(8,128)S(1)}, s32[4]{0:T(128)S(1)}, s32[4]{0:T(128)S(1)}, f32[4,3,128,128]{3,2,0,1:T(8,128)}, /*index=5*/s32[]{:T(128)}, s32[]{:T(128)}, s32[]{:T(128)}, s32[]{:T(128)}) while((s32[]{:T(128)}, f32[3,256,1024]{2,1,0:T(8,128)S(1)}, s32[4]{0:T(128)S(1)}, s32[4]{0:T(128)S(1)}, ...), condition=%wide.region_1.2_spmd, body=%wide.region_0.1_spmd.sunk | while | flops 49160 | bytes 983241 | solution.py:118
  57.9 1.1 bitcast_add_fusion.2
  59.0 2.7 dynamic_update_slice.17
  66.7 1.1 bitcast_add_fusion.2
  67.7 2.9 dynamic_update_slice.17
  75.6 1.1 bitcast_add_fusion.2
  76.6 2.9 dynamic_update_slice.17
  84.5 1.1 bitcast_add_fusion.2
  85.6 2.9 dynamic_update_slice.17
  88.5 3.8 %broadcast_in_dim.70 = f32[1,3,256,1024]{3,0,2,1:T(1,128)} reshape(f32[3,256,1024]{2,1,0:T(8,128)S(1)} %get-tuple-element.208) | data formatting | bytes 6291456 | tf_op jit(solution)/shard_map/while/body/jit(dynamic_update_index_in_dim)/broadcast_in_dim | solution.py:123
  92.3 2.6 fusion.202
  94.9 1.9 collective-permute-start.2
  96.8 2.4 collective-permute-start.3
  99.3 11.6 %collective-permute-done.2 = f32[1,3,64,1024]{3,0,2,1:T(1,128)S(1)} collective-permute-done((f32[1,3,64,1024]{3,0,2,1:T(1,128)S(1)}, f32[1,3,64,1024]{3,0,2,1:T(1,128)S(1)}, u32[]{:S(2)}, u32[]{:S(2)}) %collective-permute-start.2) | collective-permute-done | bytes 786464 | tf_op jit(solution)/shard_map/ppermute | solution.py:25
  110.9 0.9 fusion.63
  111.8 2.0 collective-permute-done.3
  115.2 1.8 divide_add_fusion
  117.8 4.9 %all-to-all-start = ((f32[1,128,1024]{2,0,1:T(1,128)}), f32[1,128,1024]{2,0,1:T(1,128)S(1)}, u32[]{:S(2)}, u32[]{:S(2)}) async-start(f32[1,128,1024]{2,0,1:T(1,128)} %slice_bitcast_fusion), calls=%async_computation | async-start | bytes 1048576 | tf_op jit(solution)/shard_map/all_to_all | solution.py:137
  123.5 131.0 %all-reduce.3.cloned.1.call-done = (f32[2,128,128]{2,1,0:T(8,128)}, f32[128,128]{1,0:T(8,128)}) async-done(((f32[2,128,128]{2,1,0:T(8,128)}, f32[128,128]{1,0:T(8,128)}), (f32[2,128,128]{2,1,0:T(8,128)}, f32[128,128]{1,0:T(8,128)})) %all-reduce.3.cloned.1.call-update) | async-done | bytes 196624 | tf_op jit(solution)/shard_map/psum | solution.py:133
  255.3 1.6 divide_add_fusion.1
  256.9 1.2 copy.70
  258.2 6.0 %fusion.53 = f32[4,32,1024]{2,1,0:T(8,128)S(1)} fusion(f32[32,4,1024]{2,0,1:T(8,128)S(1)} %bitcast.191), kind=kOutput, calls=%fused_computation.71 | convolution fusion | flops 1632632832 | bytes 1048576 | tf_op jit(solution)/shard_map/dot_general | solution.py:141
  264.2 33.6 %while.39 = (s32[]{:T(128)}, f32[32,2048]{1,0:T(8,128)S(1)}, f32[4,32,1024]{2,1,0:T(8,128)S(1)}, s32[4,2,1024]{2,1,0:T(2,128)}, f32[4,2,1024]{2,1,0:T(2,128)}, /*index=5*/s32[]{:T(128)}, s32[]{:T(128)}, s32[]{}) while((s32[]{:T(128)}, f32[32,2048]{1,0:T(8,128)S(1)}, f32[4,32,1024]{2,1,0:T(8,128)S(1)}, ...), condition=%wide.region_8.9_spmd.clone.clone, body=%wide.region_7.8_spmd.clone.clone.sunk | while | flops 815992832 | bytes 1409155 | solution.py:162
  265.8 3.3 %fusion.232 = f32[32,1024]{1,0:T(8,128)S(1)} fusion(f32[1024]{0:T(1024)S(1)} %bitcast.199, s32[1024]{0:T(1024)S(1)} %broadcast_add_fusion.6, f32[1024]{0:T(1024)S(1)} %broadcast_subtract_fusion.5, s32[1024]{0:T(1024)S(1)} %bitcast.197, f32[4,32,1024]{2,1,0:T(8,128)S(1)} %get-tuple-element.500, s32[]{:T(128)} %get-tuple-element.490), kind=kOutput, calls=%fused_computation.12.clone.1 | convolution fusion | flops 407896064 | bytes 278532 | tf_op jit(solution)/shard_map/while/body/eval_jaxpr/dot_general | solution.py:159
  269.2 3.3 %fusion.231 = f32[32,1024]{1,0:T(8,128)S(1)} fusion(f32[1024]{0:T(1024)S(1)} %bitcast.195, s32[1024]{0:T(1024)S(1)} %broadcast_add_fusion.5, f32[1024]{0:T(1024)S(1)} %broadcast_subtract_fusion.4, s32[1024]{0:T(1024)S(1)} %bitcast.193, f32[4,32,1024]{2,1,0:T(8,128)S(1)} %get-tuple-element.500, s32[]{:T(128)} %get-tuple-element.490), kind=kOutput, calls=%fused_computation.8.clone.1 | convolution fusion | flops 407896064 | bytes 278532 | tf_op jit(solution)/shard_map/while/body/eval_jaxpr/dot_general | solution.py:159
  274.2 3.3 %fusion.232 = f32[32,1024]{1,0:T(8,128)S(1)} fusion(f32[1024]{0:T(1024)S(1)} %bitcast.199, s32[1024]{0:T(1024)S(1)} %broadcast_add_fusion.6, f32[1024]{0:T(1024)S(1)} %broadcast_subtract_fusion.5, s32[1024]{0:T(1024)S(1)} %bitcast.197, f32[4,32,1024]{2,1,0:T(8,128)S(1)} %get-tuple-element.500, s32[]{:T(128)} %get-tuple-element.490), kind=kOutput, calls=%fused_computation.12.clone.1 | convolution fusion | flops 407896064 | bytes 278532 | tf_op jit(solution)/shard_map/while/body/eval_jaxpr/dot_general | solution.py:159
  277.6 3.3 %fusion.231 = f32[32,1024]{1,0:T(8,128)S(1)} fusion(f32[1024]{0:T(1024)S(1)} %bitcast.195, s32[1024]{0:T(1024)S(1)} %broadcast_add_fusion.5, f32[1024]{0:T(1024)S(1)} %broadcast_subtract_fusion.4, s32[1024]{0:T(1024)S(1)} %bitcast.193, f32[4,32,1024]{2,1,0:T(8,128)S(1)} %get-tuple-element.500, s32[]{:T(128)} %get-tuple-element.490), kind=kOutput, calls=%fused_computation.8.clone.1 | convolution fusion | flops 407896064 | bytes 278532 | tf_op jit(solution)/shard_map/while/body/eval_jaxpr/dot_general | solution.py:159
  282.6 3.3 %fusion.232 = f32[32,1024]{1,0:T(8,128)S(1)} fusion(f32[1024]{0:T(1024)S(1)} %bitcast.199, s32[1024]{0:T(1024)S(1)} %broadcast_add_fusion.6, f32[1024]{0:T(1024)S(1)} %broadcast_subtract_fusion.5, s32[1024]{0:T(1024)S(1)} %bitcast.197, f32[4,32,1024]{2,1,0:T(8,128)S(1)} %get-tuple-element.500, s32[]{:T(128)} %get-tuple-element.490), kind=kOutput, calls=%fused_computation.12.clone.1 | convolution fusion | flops 407896064 | bytes 278532 | tf_op jit(solution)/shard_map/while/body/eval_jaxpr/dot_general | solution.py:159
  285.9 3.3 %fusion.231 = f32[32,1024]{1,0:T(8,128)S(1)} fusion(f32[1024]{0:T(1024)S(1)} %bitcast.195, s32[1024]{0:T(1024)S(1)} %broadcast_add_fusion.5, f32[1024]{0:T(1024)S(1)} %broadcast_subtract_fusion.4, s32[1024]{0:T(1024)S(1)} %bitcast.193, f32[4,32,1024]{2,1,0:T(8,128)S(1)} %get-tuple-element.500, s32[]{:T(128)} %get-tuple-element.490), kind=kOutput, calls=%fused_computation.8.clone.1 | convolution fusion | flops 407896064 | bytes 278532 | tf_op jit(solution)/shard_map/while/body/eval_jaxpr/dot_general | solution.py:159
  291.0 3.3 %fusion.232 = f32[32,1024]{1,0:T(8,128)S(1)} fusion(f32[1024]{0:T(1024)S(1)} %bitcast.199, s32[1024]{0:T(1024)S(1)} %broadcast_add_fusion.6, f32[1024]{0:T(1024)S(1)} %broadcast_subtract_fusion.5, s32[1024]{0:T(1024)S(1)} %bitcast.197, f32[4,32,1024]{2,1,0:T(8,128)S(1)} %get-tuple-element.500, s32[]{:T(128)} %get-tuple-element.490), kind=kOutput, calls=%fused_computation.12.clone.1 | convolution fusion | flops 407896064 | bytes 278532 | tf_op jit(solution)/shard_map/while/body/eval_jaxpr/dot_general | solution.py:159
  294.3 3.3 %fusion.231 = f32[32,1024]{1,0:T(8,128)S(1)} fusion(f32[1024]{0:T(1024)S(1)} %bitcast.195, s32[1024]{0:T(1024)S(1)} %broadcast_add_fusion.5, f32[1024]{0:T(1024)S(1)} %broadcast_subtract_fusion.4, s32[1024]{0:T(1024)S(1)} %bitcast.193, f32[4,32,1024]{2,1,0:T(8,128)S(1)} %get-tuple-element.500, s32[]{:T(128)} %get-tuple-element.490), kind=kOutput, calls=%fused_computation.8.clone.1 | convolution fusion | flops 407896064 | bytes 278532 | tf_op jit(solution)/shard_map/while/body/eval_jaxpr/dot_general | solution.py:159
  297.8 0.9 reshape.185
  (95 shorter events, 31.9 us)
Async XLA Ops:
  7.2 18.5 %copy-start.1 = (f32[1,2,128,1024]{3,2,1,0:T(8,128)S(1)}, f32[1,2,128,1024]{3,2,1,0:T(8,128)}, u32[]{:S(2)}) copy-start(f32[1,2,128,1024]{3,2,1,0:T(8,128)} %param.17) | copy-start | bytes 3145732
  8.5 12.7 %collective-permute-start = (f32[1,2,64,1024]{3,2,1,0:T(8,128)S(1)}, f32[1,2,64,1024]{3,2,1,0:T(8,128)S(1)}, u32[]{:S(2)}, u32[]{:S(2)}) collective-permute-start(f32[1,2,64,1024]{3,2,1,0:T(8,128)S(1)} %get-tuple-element.327), channel_id=1, source_target_pairs={{0,1},{1,2},{2,3},{3,4},{4,5},{5,6},{6,7},{8,9},{9,10},{10,11},{11... | collective-permute-start | bytes 1572872 | tf_op jit(solution)/shard_map/ppermute | solution.py:14
  12.2 13.5 %collective-permute-start.1 = (f32[1,2,64,1024]{3,2,1,0:T(8,128)S(1)}, f32[1,2,64,1024]{3,2,1,0:T(8,128)}, u32[]{:S(2)}, u32[]{:S(2)}) collective-permute-start(f32[1,2,64,1024]{3,2,1,0:T(8,128)S(1)} %get-tuple-element.328), channel_id=1, source_target_pairs={{1,0},{2,1},{3,2},{4,3},{5,4},{6,5},{7,6},{9,8},{10,9},{11,10},{12... | collective-permute-start | bytes 1572872 | tf_op jit(solution)/shard_map/ppermute | solution.py:17
  21.2 0.8 copy-start.5
  37.3 7.0 %copy-start.6 = (f32[1,4,128,128]{3,2,1,0:T(8,128)S(1)}, f32[1,4,128,128]{3,2,1,0:T(8,128)}, u32[]{:S(2)}) copy-start(f32[1,4,128,128]{3,2,1,0:T(8,128)} %param.14) | copy-start | bytes 786436
  45.2 4.8 %copy-start.3 = (f32[4,2,128,128]{3,2,0,1:T(8,128)S(1)}, f32[4,2,128,128]{3,2,0,1:T(8,128)}, u32[]{:S(2)}) copy-start(f32[4,2,128,128]{3,2,0,1:T(8,128)} %get-tuple-element.217) | copy-start | bytes 1572868
  92.3 18.6 %copy-start = (f32[1,3,256,1024]{3,0,2,1:T(1,128)S(1)}, f32[1,3,256,1024]{3,0,2,1:T(1,128)}, u32[]{:S(2)}) copy-start(f32[1,3,256,1024]{3,0,2,1:T(1,128)} %broadcast_in_dim.70) | copy-start | bytes 9437188
  92.3 18.6 %slice-start = ((f32[1,3,256,1024]{3,0,2,1:T(1,128)}), f32[1,3,128,1024]{3,0,2,1:T(1,128)S(1)}, s32[]{:S(2)}) async-start(f32[1,3,256,1024]{3,0,2,1:T(1,128)} %broadcast_in_dim.70), calls=%async_computation.2 | async-start | bytes 3145728 | tf_op jit(solution)/shard_map/slice | solution.py:128
  94.9 16.0 %collective-permute-start.2 = (f32[1,3,64,1024]{3,0,2,1:T(1,128)S(1)}, f32[1,3,64,1024]{3,0,2,1:T(1,128)S(1)}, u32[]{:S(2)}, u32[]{:S(2)}) collective-permute-start(f32[1,3,64,1024]{3,0,2,1:T(1,128)S(1)} %get-tuple-element.326), channel_id=1, source_target_pairs={{0,1},{1,2},{2,3},{3,4},{4,5},{5,6},{6,7},{8,9},{9,10},{10,11},{11... | collective-permute-start | bytes 2359304 | tf_op jit(solution)/shard_map/ppermute | solution.py:25
  96.8 16.9 %collective-permute-start.3 = (f32[1,3,64,1024]{3,0,2,1:T(1,128)S(1)}, f32[1,3,64,1024]{3,0,2,1:T(1,128)S(1)}, u32[]{:S(2)}, u32[]{:S(2)}) collective-permute-start(f32[1,3,64,1024]{3,0,2,1:T(1,128)S(1)} %get-tuple-element.325), channel_id=1, source_target_pairs={{1,0},{2,1},{3,2},{4,3},{5,4},{6,5},{7,6},{9,8},{10,9},{11,10},{12... | collective-permute-start | bytes 2359304 | tf_op jit(solution)/shard_map/ppermute | solution.py:25
  99.3 15.9 %copy-start.2 = (f32[1,2,128,1024]{3,2,1,0:T(8,128)S(1)}, f32[1,2,128,1024]{3,2,1,0:T(8,128)}, u32[]{:S(2)}) copy-start(f32[1,2,128,1024]{3,2,1,0:T(8,128)} %param.17) | copy-start | bytes 3145732
  115.2 140.1 %copy-start.4 = (f32[2,128,128]{2,1,0:T(8,128)S(1)}, f32[2,128,128]{2,1,0:T(8,128)}, u32[]{:S(2)}) copy-start(f32[2,128,128]{2,1,0:T(8,128)} %param.16) | copy-start | bytes 393220
  117.8 140.2 %all-to-all-start = ((f32[1,128,1024]{2,0,1:T(1,128)}), f32[1,128,1024]{2,0,1:T(1,128)S(1)}, u32[]{:S(2)}, u32[]{:S(2)}) async-start(f32[1,128,1024]{2,0,1:T(1,128)} %slice_bitcast_fusion), calls=%async_computation | async-start | bytes 1048576 | tf_op jit(solution)/shard_map/all_to_all | solution.py:137
  122.8 131.7 %all-reduce.3.cloned.1.call-start = ((), (), s32[]{:S(2)}) async-start(), calls=%async_computation.1 | async-start | bytes 393216 | tf_op jit(solution)/shard_map/psum | solution.py:133
Sparse Core Ops, SparseCore 0:
  129.7 124.6 all-reduce.2
where the time goes:
time: 310 us; the launch traced here: 306 us
  waiting for transfers between devices  152 us (49%)
  local copies, waits for them, and re-layouts  45.8 us (15%)
  matrix products  45.6 us (15%)
  other arithmetic  17.6 us (6%)
  loops' own time  15.4 us (5%)
  starting transfers between devices  14.9 us (5%)
  between operations  14.4 us (5%)
    psum x1, waiting for transfers between devices, on_device(): lax.psum((jnp.sum(numers, axis=0), jnp.sum(denoms, axis=0)), ('angle', 'p...  131 us
    dot_general x8, matrix products, back_step(): results.append(jnp.dot(rows_angle, matrix, precision=lax.Precision.HIGHEST))  26.6 us
    another operation x1, loops' own time, one_angle(): lax.fori_loop(0, per_device, accumulate, jnp.zeros((channels, band + patc...  15.2 us
    ppermute x2, waiting for transfers between devices, passed_along(): return lax.ppermute(array, axis, pairs)  13.6 us
    dynamic_update_slice x4, local copies, waits for them, and re-layouts, accumulate(): return lax.dynamic_update_slice(total, current + stacked[count], start)  11.4 us
    gather x12, local copies, waits for them, and re-layouts  10.2 us
  transfers between devices with their start and end apart: 6, of which 5 were waited for; matrix products, arithmetic and copies ran while one was open for 3% of the time, Pallas kernels for 0%

commit v1 on v0

v1 whole, which is shorter than its diff:
```python
import math

import numpy as np
import jax
import jax.numpy as jnp
from jax import lax
from jax.experimental import pallas as pl
from jax.experimental.pallas import tpu as pltpu
from jax.sharding import PartitionSpec as P

LANES = 128
ROWS = 8
BINS = 256


def passed_along(array, axis, by):
    length = lax.axis_size(axis)
    pairs = [(i, i + by) for i in range(length) if 0 <= i + by < length]
    return lax.ppermute(array, axis, pairs)


def split_halves(value):
    high = value.astype(jnp.bfloat16)
    low = (value - high.astype(jnp.float32)).astype(jnp.bfloat16)
    return high, low


def dft_tables(length):
    phases = np.outer(np.arange(length), np.arange(length)) % length
    theta = phases * (2.0 * math.pi / length)
    real = np.cos(theta) / math.sqrt(length)
    imag = -np.sin(theta) / math.sqrt(length)
    table = np.block([[real, imag], [-imag, real]]).astype(np.float32)
    tables = []
    for each in (table, table.T):
        high = each.astype(jnp.bfloat16)
        low = (each - high.astype(np.float32)).astype(jnp.bfloat16)
        tables += [high, low]
    return np.stack(tables)


def product(left, right):
    (left_high, left_low), (right_high, right_low) = left, right

    def dot(a, b):
        return jnp.dot(a, b, preferred_element_type=jnp.float32)

    return dot(left_high, right_high) + (dot(left_high, right_low) + dot(left_low, right_high))


def gradient_kernel(places, low_ref, block_ref, high_ref, probe_ref, amp_ref, table_ref,
                    up_ref, own_ref, down_ref, stat_ref, field, total):
    count, patch = amp_ref.shape[0], amp_ref.shape[1]
    half, band, width = low_ref.shape[1], block_ref.shape[1], block_ref.shape[2]
    field[:, :half] = low_ref[...]
    field[:, half:half + band] = block_ref[...]
    field[:, half + band:] = high_ref[...]
    total[...] = jnp.zeros(total.shape, jnp.float32)
    probe_real = probe_ref[0]
    probe_imag = probe_ref[1]
    power = probe_real * probe_real + probe_imag * probe_imag
    window = patch + LANES
    tall = patch + ROWS
    last = (width - window) // LANES
    spots = []
    patches = []
    waves = []
    for b in range(count):
        row = places[b, 0]
        col = places[b, 1]
        top = pl.multiple_of(row // ROWS * ROWS, ROWS)
        base = pl.multiple_of(jnp.minimum(col // LANES, last) * LANES, LANES)
        drop = row - top
        shift = col - base
        spots.append((top, drop, base, shift))
        cut = []
        for ch in range(2):
            wide = field[ch, pl.ds(top, tall), pl.ds(base, window)]
            narrow = pltpu.roll(wide, lax.rem(window - shift, window), 1)[:, :patch]
            cut.append(pltpu.roll(narrow, lax.rem(tall - drop, tall), 0)[:patch])
        patches.append(cut)
        waves.append((probe_real * cut[0] - probe_imag * cut[1], probe_real * cut[1] + probe_imag * cut[0]))
    forward = (table_ref[0], table_ref[1])
    backward = (table_ref[2], table_ref[3])

    def by_rows(pairs):
        return jnp.concatenate([jnp.concatenate(pair, axis=1) for pair in pairs], axis=0)

    def by_columns(pairs):
        return jnp.concatenate([jnp.concatenate(pair, axis=0) for pair in pairs], axis=1)

    def from_rows(whole):
        return [(whole[b * patch:(b + 1) * patch, :patch], whole[b * patch:(b + 1) * patch, patch:]) for b in range(count)]

    def from_columns(whole):
        return [(whole[:patch, b * patch:(b + 1) * patch], whole[patch:, b * patch:(b + 1) * patch]) for b in range(count)]

    middle = from_rows(product(split_halves(by_rows(waves)), forward))
    spectra = from_columns(product(backward, split_halves(by_columns(middle))))
    fixed = []
    for b in range(count):
        real, imag = spectra[b]
        factor = amp_ref[b] / jnp.maximum(jnp.sqrt(real * real + imag * imag), 0.5)
        fixed.append((factor * real, factor * imag))
    middle = from_columns(product(forward, split_halves(by_columns(fixed))))
    back = from_rows(product(split_halves(by_rows(middle)), backward))
    numer_real = jnp.zeros((patch, patch), jnp.float32)
    numer_imag = jnp.zeros((patch, patch), jnp.float32)
    denom = jnp.zeros((patch, patch), jnp.float32)
    blank = jnp.zeros((tall, LANES), jnp.float32)
    blank_rows = jnp.zeros((ROWS, patch), jnp.float32)
    for b in range(count):
        top, drop, base, shift = spots[b]
        cut_real, cut_imag = patches[b]
        diff_real = back[b][0] - waves[b][0]
        diff_imag = back[b][1] - waves[b][1]
        numer_real += cut_real * diff_real + cut_imag * diff_imag
        numer_imag += cut_real * diff_imag - cut_imag * diff_real
        denom += cut_real * cut_real + cut_imag * cut_imag
        terms = (probe_real * diff_real + probe_imag * diff_imag,
                 probe_real * diff_imag - probe_imag * diff_real, power)
        for ch, term in enumerate(terms):
            tall_term = pltpu.roll(jnp.concatenate([term, blank_rows], axis=0), drop, 0)
            wide = pltpu.roll(jnp.concatenate([tall_term, blank], axis=1), shift, 1)
            spot = (ch, pl.ds(top, tall), pl.ds(base, window))
            total[spot] = total[spot] + wide
    stat_ref[0] = numer_real
    stat_ref[1] = numer_imag
    stat_ref[2] = denom
    up_ref[...] = total[:, :half]
    own_ref[...] = total[:, half:half + band]
    down_ref[...] = total[:, half + band:]


def update_kernel(object_ref, own_ref, above_ref, below_ref, out_ref, imag_ref):
    band = own_ref.shape[1]
    half = above_ref.shape[1]
    ends = sorted({0, half, band - half, band})
    for start, stop in zip(ends[:-1], ends[1:]):
        terms = [own_ref[ch, start:stop] for ch in range(3)]
        if stop <= half:
            terms = [terms[ch] + above_ref[ch, start:stop] for ch in range(3)]
        if start >= band - half:
            offset = band - half
            terms = [terms[ch] + below_ref[ch, start - offset:stop - offset] for ch in range(3)]
        scale = terms[2] + 1.0
        out_ref[0, start:stop] = object_ref[0, start:stop] + terms[0] / scale
        imag = object_ref[1, start:stop] + terms[1] / scale
        out_ref[1, start:stop] = imag
        imag_ref[start:stop] = imag


def ramp_kernel(high_ref, low_ref):
    rows, width = high_ref.shape
    line = lax.broadcasted_iota(jnp.int32, (rows, width), 0) + pl.program_id(0) * rows
    differ = line - lax.broadcasted_iota(jnp.int32, (rows, width), 1)
    spread = differ.astype(jnp.float32)
    squared = jnp.maximum(spread * spread, 1.0)
    odd_terms = jnp.where((differ & 1) != 0, (-1.0 / (math.pi * math.pi)) / squared, 0.0)
    high, low = split_halves(jnp.where(differ == 0, 0.25, odd_terms))
    high_ref[...] = high
    low_ref[...] = low


def back_kernel(sino_ref, ramp_high_ref, ramp_low_ref, index_ref, weight_ref, out_ref, parts):
    angles, rows, width = sino_ref.shape
    depth = index_ref.shape[1]
    columns = index_ref.shape[2]

    @pl.when(pl.program_id(0) == 0)
    def _():
        sino = sino_ref[...].reshape(angles * rows, width)
        filtered = product(split_halves(sino), (ramp_high_ref[...], ramp_low_ref[...])) * (math.pi / angles)
        change = pltpu.roll(filtered, width - 1, 1) - filtered
        pieces = split_halves(filtered) + split_halves(change)
        for a in range(angles):
            for i in range(4):
                parts[a, i * rows:(i + 1) * rows] = pieces[i][a * rows:(a + 1) * rows]

    bins = lax.broadcasted_iota(jnp.int32, (width, columns), 0)
    for z in range(depth):
        result = jnp.zeros((rows, columns), jnp.float32)
        for a in range(angles):
            chosen = jnp.where(bins == index_ref[a, z:z + 1, :], 1.0, 0.0).astype(jnp.bfloat16)
            got = jnp.dot(parts[a], chosen, preferred_element_type=jnp.float32)
            lower = got[:rows] + got[rows:2 * rows]
            rise = got[2 * rows:3 * rows] + got[3 * rows:]
            result += lower + weight_ref[a, z:z + 1, :] * rise
        out_ref[:, z, :] = result


def on_device(amplitude, offsets, probe_field, object_field, interp_index, interp_weight):
    f32 = jnp.float32
    band = object_field.shape[2]
    width = object_field.shape[3]
    patch = probe_field.shape[1]
    half = patch // 2
    vmem = pl.BlockSpec(memory_space=pltpu.VMEM)
    smem = pl.BlockSpec(memory_space=pltpu.SMEM)
    layer = object_field[0]
    low = passed_along(layer[:, band - half:], "pos", 1)
    high = passed_along(layer[:, :half], "pos", -1)
    anchor = lax.axis_index("pos") * band - half
    places = offsets[0] - jnp.stack([anchor, 0]).astype(jnp.int32)
    up, own, down, stats = pl.pallas_call(
        gradient_kernel,
        name="gradient",
        out_shape=(
            jax.ShapeDtypeStruct((3, half, width), f32),
            jax.ShapeDtypeStruct((3, band, width), f32),
            jax.ShapeDtypeStruct((3, half, width), f32),
            jax.ShapeDtypeStruct((3, patch, patch), f32),
        ),
        in_specs=[smem] + [vmem] * 6,
        out_specs=[vmem] * 4,
        scratch_shapes=[pltpu.VMEM((2, band + patch, width), f32), pltpu.VMEM((3, band + patch, width), f32)],
    )(places, low, layer, high, probe_field, amplitude[0], dft_tables(patch))
    from_below = passed_along(up, "pos", -1)
    from_above = passed_along(down, "pos", 1)
    ramp_rows = width // 4
    ramp_high, ramp_low = pl.pallas_call(
        ramp_kernel,
        name="ramp",
        grid=(width // ramp_rows,),
        out_shape=(jax.ShapeDtypeStruct((width, width), jnp.bfloat16),) * 2,
        out_specs=[pl.BlockSpec((ramp_rows, width), lambda i: (i, 0))] * 2,
        cost_estimate=pl.CostEstimate(flops=20 * width * width, transcendentals=0, bytes_accessed=4 * width * width),
    )()
    new_layer, imag = pl.pallas_call(
        update_kernel,
        name="update",
        out_shape=(jax.ShapeDtypeStruct((2, band, width), f32), jax.ShapeDtypeStruct((band, width), f32)),
        in_specs=[vmem] * 4,
        out_specs=[vmem] * 2,
    )(layer, own, from_above, from_below)
    everyone = ("angle", "pos")
    shares = lax.axis_size("angle") * lax.axis_size("pos")
    angles = lax.axis_size("angle")
    regrouped = lax.all_to_all(imag.reshape(angles, band // angles, width), "angle", split_axis=0, concat_axis=0, tiled=True)
    pieces = jnp.swapaxes(stats.reshape(3, shares, -1), 0, 1)
    mine = jnp.sum(lax.all_to_all(pieces, everyone, split_axis=0, concat_axis=0, tiled=True), axis=0)
    step = mine[:2] / (mine[2:] + 1.0)
    steps = lax.all_gather(step, everyone, axis=0, tiled=False)
    new_probe = probe_field + jnp.swapaxes(steps, 0, 1).reshape(probe_field.shape)
    rows = band // angles
    zwin = interp_index.shape[1]
    columns = min(BINS, width)
    recon = pl.pallas_call(
        back_kernel,
        name="back",
        grid=(width // columns,),
        out_shape=jax.ShapeDtypeStruct((rows, zwin, width), f32),
        in_specs=[
            pl.BlockSpec((angles, rows, width), lambda i: (0, 0, 0)),
            pl.BlockSpec((width, width), lambda i: (0, 0)),
            pl.BlockSpec((width, width), lambda i: (0, 0)),
            pl.BlockSpec((angles, zwin, columns), lambda i: (0, 0, i)),
            pl.BlockSpec((angles, zwin, columns), lambda i: (0, 0, i)),
        ],
        out_specs=pl.BlockSpec((rows, zwin, columns), lambda i: (0, 0, i)),
        scratch_shapes=[pltpu.VMEM((angles, 4 * rows, width), jnp.bfloat16)],
        compiler_params=pltpu.CompilerParams(dimension_semantics=("arbitrary",)),
    )(regrouped, ramp_high, ramp_low, interp_index, interp_weight)
    return (new_layer[None], new_probe, recon[None])


def solution(mesh):
    placed = (
        P("angle", "pos", None, None),
        P("angle", "pos", None),
        P(),
        P("angle", None, "pos", None),
        P(),
        P(),
    )
    return jax.shard_map(
        on_device,
        mesh=mesh,
        in_specs=placed,
        out_specs=(P("angle", None, "pos", None), P(), P("pos", "angle", None, None)),
        check_vma=False,
    )
```

time: 310 us -> 112 us (0.36)
  waiting for transfers between devices: 152 us -> 19.5 us
  matrix products: 45.6 us -> 0 us
  local copies, waits for them, and re-layouts: 45.8 us -> 5.89 us
  blocking collectives: 0 us -> 38.5 us
  Pallas kernels: 0 us -> 20.7 us
  other arithmetic: 17.6 us -> 1.41 us
  loops' own time: 15.4 us -> 0 us
  between operations: 14.4 us -> 0.73 us
  starting transfers between devices: 14.9 us -> 23.7 us
    psum x1 -> x0, waiting for transfers between devices: 131 us -> none  [on_device(): lax.psum((jnp.sum(numers, axis=0), jnp.sum(denoms, axis=0)), ('angle', 'p...]
    dot_general x25 -> x0, matrix products: 45.6 us -> none  [the longest x8 26.6 us: back_step(): results.append(jnp.dot(rows_angle, matrix, precision=lax.Precision.HIGHEST))]
    all_gather x0 -> x1, blocking collectives: none -> 38.5 us  [on_device(): steps = lax.all_gather(step, everyone, axis=0, tiled=False)]
    pallas_call x0 -> x4, Pallas kernels: none -> 20.7 us  [the longest x1 7.31 us: on_device(): pl.pallas_call(back_kernel, name='back', grid=(width // columns,), out_sh...]
    another operation x3 -> x0, loops' own time: 15.4 us -> none  [the longest x1 15.2 us: one_angle(): lax.fori_loop(0, per_device, accumulate, jnp.zeros((channels, band + patc...]
    dynamic_update_slice x4 -> x0, local copies, waits for them, and re-layouts: 11.4 us -> none  [accumulate(): return lax.dynamic_update_slice(total, current + stacked[count], start)]
    add x22 -> x2, other arithmetic: 11.3 us -> 0.68 us  [the longest x1 0.67 us: on_device(): probe_field + jnp.swapaxes(steps, 0, 1).reshape(probe_field.shape)]
    gather x12 -> x0, local copies, waits for them, and re-layouts: 10.2 us -> none
  transfers between devices with their start and end apart: 6 -> 6, of which waited for: 5 -> 3; matrix products, arithmetic and copies ran while one was open for 3% -> 3% of each run, Pallas kernels for 0% -> 6%
where the time goes in v1:
time: 112 us; the launch traced here: 110 us
  blocking collectives  38.5 us (34%)
  starting transfers between devices  23.7 us (21%)
  Pallas kernels  20.7 us (18%)
  waiting for transfers between devices  19.5 us (17%)
  local copies, waits for them, and re-layouts  5.89 us (5%)
  other arithmetic  1.41 us (1%)
    all_gather x1, blocking collectives, on_device(): steps = lax.all_gather(step, everyone, axis=0, tiled=False)  38.5 us
    ppermute x4, waiting for transfers between devices, passed_along(): return lax.ppermute(array, axis, pairs)  19.5 us
    ppermute x4, starting transfers between devices, passed_along(): return lax.ppermute(array, axis, pairs)  12.9 us
    pallas_call x1, Pallas kernels, on_device(): pl.pallas_call(back_kernel, name='back', grid=(width // columns,), out_sh...  7.31 us
    pallas_call x1, Pallas kernels, on_device(): pl.pallas_call(gradient_kernel, name='gradient', out_shape=(jax.ShapeDtyp...  6.42 us
    all_to_all x1, starting transfers between devices, on_device(): lax.all_to_all(pieces, everyone, split_axis=0, concat_axis=0, tiled=True)  6.33 us
    all_to_all x1, starting transfers between devices, on_device(): lax.all_to_all(imag.reshape(angles, band // angles, width), 'angle', spli...  4.44 us
    pallas_call x1, Pallas kernels, on_device(): pl.pallas_call(update_kernel, name='update', out_shape=(jax.ShapeDtypeStr...  3.56 us
  transfers between devices with their start and end apart: 6, of which 3 were waited for; matrix products, arithmetic and copies ran while one was open for 3% of the time, Pallas kernels for 6%

profile of v1, /device:TPU:3, one launch (start us, length us, event | category | flops | bytes accessed | tf_op | source)
XLA Modules:
  0.0 110.4 jit_solution(13330032164183196038)
XLA Ops:
  0.6 0.0 copy-start.6
  0.6 1.3 %fusion.1 = (f32[2,64,1024]{2,1,0:T(8,128)S(1)}, f32[2,64,1024]{2,1,0:T(8,128)S(1)}) fusion(f32[2,128,1024]{2,1,0:T(8,128)} %bitcast.14), kind=kLoop, calls=%fused_computation.6 | loop fusion | bytes 2097152 | tf_op jit(solution)/shard_map/slice | solution.py:202
  1.9 2.6 %collective-permute-start.1 = (f32[2,64,1024]{2,1,0:T(8,128)S(1)}, f32[2,64,1024]{2,1,0:T(8,128)S(1)}, u32[]{:S(2)}, u32[]{:S(2)}) collective-permute-start(f32[2,64,1024]{2,1,0:T(8,128)S(1)} %get-tuple-element.19), channel_id=1, source_target_pairs={{1,0},{2,1},{3,2},{4,3},{5,4},{6,5},{7,6},{9,8},{10,9},{11,10},{12... | collective-permute-start | bytes 1572872 | tf_op jit(solution)/shard_map/ppermute | solution.py:19
  4.5 3.9 %collective-permute-start = (f32[2,64,1024]{2,1,0:T(8,128)S(1)}, f32[2,64,1024]{2,1,0:T(8,128)S(1)}, u32[]{:S(2)}, u32[]{:S(2)}) collective-permute-start(f32[2,64,1024]{2,1,0:T(8,128)S(1)} %get-tuple-element.20), channel_id=1, source_target_pairs={{0,1},{1,2},{2,3},{3,4},{4,5},{5,6},{6,7},{8,9},{9,10},{10,11},{11... | collective-permute-start | bytes 1572872 | tf_op jit(solution)/shard_map/ppermute | solution.py:19
  8.4 0.0 copy-done.6
  8.4 0.1 copy.13
  8.5 0.1 pad_add_fusion
  8.6 0.6 broadcast_subtract_fusion.places
  9.2 7.8 %collective-permute-done.1.high_ref = f32[2,64,1024]{2,1,0:T(8,128)S(1)} collective-permute-done((f32[2,64,1024]{2,1,0:T(8,128)S(1)}, f32[2,64,1024]{2,1,0:T(8,128)S(1)}, u32[]{:S(2)}, u32[]{:S(2)}) %collective-permute-start.1) | collective-permute-done | bytes 524320 | tf_op jit(solution)/shard_map/ppermute | solution.py:19
  17.0 0.0 copy-start.3
  17.0 0.0 collective-permute-done.low_ref
  17.0 0.0 copy-start.4
  17.0 0.8 copy-done.3
  17.8 0.2 copy-done.4
  17.9 6.4 %gradient.1 = (f32[3,64,1024]{2,1,0:T(8,128)}, f32[3,128,1024]{2,1,0:T(8,128)}, f32[3,64,1024]{2,1,0:T(8,128)}, f32[3,128,128]{2,1,0:T(8,128)}) custom-call(s32[4,2]{1,0:T(4,128)} %broadcast_subtract_fusion.places, f32[2,64,1024]{2,1,0:T(8,128)} %copy-done.4, f32[2,128,1024]{2,1,0:T(8,128)} %bitcast.15, f32[2,64,1024]{2,1,0:T(8,128)} %copy-done.3, ...), custom_call_target="tpu_custom_call" | custom-call | tf_op jit(solution)/shard_map/gradient/pallas_call | solution.py:205
  24.4 4.6 %collective-permute-start.2 = (f32[3,64,1024]{2,1,0:T(8,128)}, f32[3,64,1024]{2,1,0:T(8,128)S(1)}, u32[]{:S(2)}, u32[]{:S(2)}) collective-permute-start(f32[3,64,1024]{2,1,0:T(8,128)} %get-tuple-element.12), channel_id=1, source_target_pairs={{0,1},{1,2},{2,3},{3,4},{4,5},{5,6},{6,7},{8,9},{9,10},{10,11},{11... | collective-permute-start | bytes 2359304 | tf_op jit(solution)/shard_map/ppermute | solution.py:19
  28.9 1.9 %collective-permute-start.3 = (f32[3,64,1024]{2,1,0:T(8,128)}, f32[3,64,1024]{2,1,0:T(8,128)S(1)}, u32[]{:S(2)}, u32[]{:S(2)}) collective-permute-start(f32[3,64,1024]{2,1,0:T(8,128)} %get-tuple-element.13), channel_id=1, source_target_pairs={{1,0},{2,1},{3,2},{4,3},{5,4},{6,5},{7,6},{9,8},{10,9},{11,10},{12... | collective-permute-start | bytes 2359304 | tf_op jit(solution)/shard_map/ppermute | solution.py:19
  30.9 1.0 reshape.16
  31.8 0.8 copy.17
  32.7 6.3 %all-to-all-start = ((f32[32,3,512]{2,1,0:T(4,128)}), f32[32,3,512]{2,1,0:T(4,128)S(1)}, u32[]{:S(2)}, u32[]{:S(2)}) async-start(f32[32,3,512]{2,1,0:T(4,128)} %bitcast.13), calls=%async_computation | async-start | bytes 524288 | tf_op jit(solution)/shard_map/all_to_all | solution.py:241
  39.0 9.7 %collective-permute-done.2.above_ref = f32[3,64,1024]{2,1,0:T(8,128)S(1)} collective-permute-done((f32[3,64,1024]{2,1,0:T(8,128)}, f32[3,64,1024]{2,1,0:T(8,128)S(1)}, u32[]{:S(2)}, u32[]{:S(2)}) %collective-permute-start.2) | collective-permute-done | bytes 786464 | tf_op jit(solution)/shard_map/ppermute | solution.py:19
  48.7 0.0 copy-start.1
  48.7 2.0 %collective-permute-done.3.below_ref = f32[3,64,1024]{2,1,0:T(8,128)S(1)} collective-permute-done((f32[3,64,1024]{2,1,0:T(8,128)}, f32[3,64,1024]{2,1,0:T(8,128)S(1)}, u32[]{:S(2)}, u32[]{:S(2)}) %collective-permute-start.3) | collective-permute-done | bytes 786464 | tf_op jit(solution)/shard_map/ppermute | solution.py:19
  50.7 0.0 copy-start.2
  50.7 0.0 copy-done.1
  50.7 0.9 copy-done.2
  51.6 0.0 copy-start.5
  51.6 3.6 %update.1 = (f32[2,128,1024]{2,1,0:T(8,128)}, f32[128,1024]{1,0:T(8,128)}) custom-call(f32[2,128,1024]{2,1,0:T(8,128)} %bitcast.16, f32[3,128,1024]{2,1,0:T(8,128)} %get-tuple-element.11.own_ref, f32[3,64,1024]{2,1,0:T(8,128)} %copy-done.1, f32[3,64,1024]{2,1,0:T(8,128)} %copy-done.2), custom_call_target="tpu_custom_call" | custom-call | tf_op jit(solution)/shard_map/update/pallas_call | solution.py:229
  55.2 0.0 all-to-all-done
  55.2 4.4 %all-to-all-start.1 = ((f32[4,32,1024]{2,1,0:T(8,128)}), f32[4,32,1024]{2,1,0:T(8,128)S(1)}, u32[]{:S(2)}, u32[]{:S(2)}) async-start(f32[4,32,1024]{2,1,0:T(8,128)} %bitcast.17), calls=%async_computation.1 | async-start | bytes 1048576 | tf_op jit(solution)/shard_map/all_to_all | solution.py:239
  59.6 3.4 %ramp.1 = (bf16[1024,1024]{1,0:T(8,128)(2,1)}, bf16[1024,1024]{1,0:T(8,128)(2,1)}) custom-call(), custom_call_target="tpu_custom_call" | custom-call | flops 20971520 | bytes 4194304 | tf_op jit(solution)/shard_map/ramp/pallas_call | solution.py:221
  63.0 0.1 reduce_sum.9
  63.1 38.5 %all-gather.1 = f32[32,2,512]{2,1,0:T(2,128)S(1)} all-gather(f32[1,2,512]{2,1,0:T(2,128)S(1)} %fusion), channel_id=2, replica_groups=mesh['angle'=4,'pos'=8] {'angle','pos'}, dimensions={0}, use_global_device_ids=true | all-gather | bytes 135168 | tf_op jit(solution)/shard_map/all_gather | solution.py:243
  101.6 0.0 copy-done.5
  101.6 0.7 add.12
  102.3 0.0 all-to-all-done.1.sino_ref
  102.3 0.0 copy-start
  102.3 0.8 copy-done
  103.1 7.3 %back.1 = f32[32,2,1024]{2,1,0:T(2,128)} custom-call(f32[4,32,1024]{2,1,0:T(8,128)} %copy-done, bf16[1024,1024]{1,0:T(8,128)(2,1)} %get-tuple-element.17.ramp_high_ref, bf16[1024,1024]{1,0:T(8,128)(2,1)} %get-tuple-element.18.ramp_low_ref, s32[4,2,1024]{2,1,0:T(2,128)} %index_ref.1, f32[4,2,1024]{2,1,0:T(2,128)} %weight_ref.1), custom_call_target="tpu_custom_call" | custom-call | tf_op jit(solution)/shard_map/back/pallas_call | solution.py:248
  (4 shorter events, 0.1 us)
Async XLA Ops:
  0.6 7.8 %copy-start.6 = (s32[1,4,2]{1,2,0:T(2,128)S(1)}, s32[1,4,2]{1,2,0:T(2,128)}, u32[]{:S(2)}) copy-start(s32[1,4,2]{1,2,0:T(2,128)} %param.8) | copy-start | bytes 100
  1.9 15.0 %collective-permute-start.1 = (f32[2,64,1024]{2,1,0:T(8,128)S(1)}, f32[2,64,1024]{2,1,0:T(8,128)S(1)}, u32[]{:S(2)}, u32[]{:S(2)}) collective-permute-start(f32[2,64,1024]{2,1,0:T(8,128)S(1)} %get-tuple-element.19), channel_id=1, source_target_pairs={{1,0},{2,1},{3,2},{4,3},{5,4},{6,5},{7,6},{9,8},{10,9},{11,10},{12... | collective-permute-start | bytes 1572872 | tf_op jit(solution)/shard_map/ppermute | solution.py:19
  4.5 12.5 %collective-permute-start = (f32[2,64,1024]{2,1,0:T(8,128)S(1)}, f32[2,64,1024]{2,1,0:T(8,128)S(1)}, u32[]{:S(2)}, u32[]{:S(2)}) collective-permute-start(f32[2,64,1024]{2,1,0:T(8,128)S(1)} %get-tuple-element.20), channel_id=1, source_target_pairs={{0,1},{1,2},{2,3},{3,4},{4,5},{5,6},{6,7},{8,9},{9,10},{10,11},{11... | collective-permute-start | bytes 1572872 | tf_op jit(solution)/shard_map/ppermute | solution.py:19
  17.0 0.8 copy-start.3
  17.0 1.0 copy-start.4
  24.4 24.3 %collective-permute-start.2 = (f32[3,64,1024]{2,1,0:T(8,128)}, f32[3,64,1024]{2,1,0:T(8,128)S(1)}, u32[]{:S(2)}, u32[]{:S(2)}) collective-permute-start(f32[3,64,1024]{2,1,0:T(8,128)} %get-tuple-element.12), channel_id=1, source_target_pairs={{0,1},{1,2},{2,3},{3,4},{4,5},{5,6},{6,7},{8,9},{9,10},{10,11},{11... | collective-permute-start | bytes 2359304 | tf_op jit(solution)/shard_map/ppermute | solution.py:19
  28.9 21.8 %collective-permute-start.3 = (f32[3,64,1024]{2,1,0:T(8,128)}, f32[3,64,1024]{2,1,0:T(8,128)S(1)}, u32[]{:S(2)}, u32[]{:S(2)}) collective-permute-start(f32[3,64,1024]{2,1,0:T(8,128)} %get-tuple-element.13), channel_id=1, source_target_pairs={{1,0},{2,1},{3,2},{4,3},{5,4},{6,5},{7,6},{9,8},{10,9},{11,10},{12... | collective-permute-start | bytes 2359304 | tf_op jit(solution)/shard_map/ppermute | solution.py:19
  32.7 22.5 %all-to-all-start = ((f32[32,3,512]{2,1,0:T(4,128)}), f32[32,3,512]{2,1,0:T(4,128)S(1)}, u32[]{:S(2)}, u32[]{:S(2)}) async-start(f32[32,3,512]{2,1,0:T(4,128)} %bitcast.13), calls=%async_computation | async-start | bytes 524288 | tf_op jit(solution)/shard_map/all_to_all | solution.py:241
  48.7 2.0 %copy-start.1 = (f32[3,64,1024]{2,1,0:T(8,128)}, f32[3,64,1024]{2,1,0:T(8,128)S(1)}, u32[]{:S(2)}) copy-start(f32[3,64,1024]{2,1,0:T(8,128)S(1)} %collective-permute-done.2.above_ref) | copy-start | bytes 2359300
  50.7 0.9 copy-start.2
  51.6 50.0 %copy-start.5 = (f32[2,128,128]{2,1,0:T(8,128)S(1)}, f32[2,128,128]{2,1,0:T(8,128)}, u32[]{:S(2)}) copy-start(f32[2,128,128]{2,1,0:T(8,128)} %probe_ref.1) | copy-start | bytes 393220
  55.2 47.2 %all-to-all-start.1 = ((f32[4,32,1024]{2,1,0:T(8,128)}), f32[4,32,1024]{2,1,0:T(8,128)S(1)}, u32[]{:S(2)}, u32[]{:S(2)}) async-start(f32[4,32,1024]{2,1,0:T(8,128)} %bitcast.17), calls=%async_computation.1 | async-start | bytes 1048576 | tf_op jit(solution)/shard_map/all_to_all | solution.py:239
  102.3 0.8 copy-start

commit v2 on v1

--- a/solution.py
+++ b/solution.py
@@ -48,7 +48,7 @@
     return dot(left_high, right_high) + (dot(left_high, right_low) + dot(left_low, right_high))
 
 
-def gradient_kernel(places, low_ref, block_ref, high_ref, probe_ref, amp_ref, table_ref,
+def gradient_kernel(places, low_ref, block_ref, high_ref, probe_ref, amp_ref, table_ref, ramp_ref,
                     up_ref, own_ref, down_ref, stat_ref, field, total):
     count, patch = amp_ref.shape[0], amp_ref.shape[1]
     half, band, width = low_ref.shape[1], block_ref.shape[1], block_ref.shape[2]
@@ -124,9 +124,9 @@
             wide = pltpu.roll(jnp.concatenate([tall_term, blank], axis=1), shift, 1)
             spot = (ch, pl.ds(top, tall), pl.ds(base, window))
             total[spot] = total[spot] + wide
-    stat_ref[0] = numer_real
-    stat_ref[1] = numer_imag
-    stat_ref[2] = denom
+    stat_ref[:, 0, :] = numer_real
+    stat_ref[:, 1, :] = numer_imag
+    stat_ref[:, 2, :] = denom
     up_ref[...] = total[:, :half]
     own_ref[...] = total[:, half:half + band]
     down_ref[...] = total[:, half + band:]
@@ -202,21 +202,6 @@
     high = passed_along(layer[:, :half], "pos", -1)
     anchor = lax.axis_index("pos") * band - half
     places = offsets[0] - jnp.stack([anchor, 0]).astype(jnp.int32)
-    up, own, down, stats = pl.pallas_call(
-        gradient_kernel,
-        name="gradient",
-        out_shape=(
-            jax.ShapeDtypeStruct((3, half, width), f32),
-            jax.ShapeDtypeStruct((3, band, width), f32),
-            jax.ShapeDtypeStruct((3, half, width), f32),
-            jax.ShapeDtypeStruct((3, patch, patch), f32),
-        ),
-        in_specs=[smem] + [vmem] * 6,
-        out_specs=[vmem] * 4,
-        scratch_shapes=[pltpu.VMEM((2, band + patch, width), f32), pltpu.VMEM((3, band + patch, width), f32)],
-    )(places, low, layer, high, probe_field, amplitude[0], dft_tables(patch))
-    from_below = passed_along(up, "pos", -1)
-    from_above = passed_along(down, "pos", 1)
     ramp_rows = width // 4
     ramp_high, ramp_low = pl.pallas_call(
         ramp_kernel,
@@ -226,6 +211,21 @@
         out_specs=[pl.BlockSpec((ramp_rows, width), lambda i: (i, 0))] * 2,
         cost_estimate=pl.CostEstimate(flops=20 * width * width, transcendentals=0, bytes_accessed=4 * width * width),
     )()
+    up, own, down, stats = pl.pallas_call(
+        gradient_kernel,
+        name="gradient",
+        out_shape=(
+            jax.ShapeDtypeStruct((3, half, width), f32),
+            jax.ShapeDtypeStruct((3, band, width), f32),
+            jax.ShapeDtypeStruct((3, half, width), f32),
+            jax.ShapeDtypeStruct((patch, 3, patch), f32),
+        ),
+        in_specs=[smem] + [vmem] * 6 + [pl.BlockSpec(memory_space=pl.ANY)],
+        out_specs=[vmem] * 4,
+        scratch_shapes=[pltpu.VMEM((2, band + patch, width), f32), pltpu.VMEM((3, band + patch, width), f32)],
+    )(places, low, layer, high, probe_field, amplitude[0], dft_tables(patch), ramp_high)
+    from_below = passed_along(up, "pos", -1)
+    from_above = passed_along(down, "pos", 1)
     new_layer, imag = pl.pallas_call(
         update_kernel,
         name="update",
@@ -237,11 +237,12 @@
     shares = lax.axis_size("angle") * lax.axis_size("pos")
     angles = lax.axis_size("angle")
     regrouped = lax.all_to_all(imag.reshape(angles, band // angles, width), "angle", split_axis=0, concat_axis=0, tiled=True)
-    pieces = jnp.swapaxes(stats.reshape(3, shares, -1), 0, 1)
+    pieces = stats.reshape(shares, patch // shares, 3, patch)
     mine = jnp.sum(lax.all_to_all(pieces, everyone, split_axis=0, concat_axis=0, tiled=True), axis=0)
-    step = mine[:2] / (mine[2:] + 1.0)
-    steps = lax.all_gather(step, everyone, axis=0, tiled=False)
-    new_probe = probe_field + jnp.swapaxes(steps, 0, 1).reshape(probe_field.shape)
+    step = mine[:, :2] / (mine[:, 2:] + 1.0)
+    copies = jnp.broadcast_to(step[None], (shares,) + step.shape)
+    steps = lax.all_to_all(copies, everyone, split_axis=0, concat_axis=0, tiled=True)
+    new_probe = probe_field + jnp.swapaxes(steps.reshape(patch, 2, patch), 0, 1)
     rows = band // angles
     zwin = interp_index.shape[1]
     columns = min(BINS, width)

time: 112 us -> 89.2 us (0.80)
  blocking collectives: 38.5 us -> 0 us
  waiting for transfers between devices: 19.5 us -> 32.7 us
  starting transfers between devices: 23.7 us -> 26.6 us
    all_gather x1 -> x0, blocking collectives: 38.5 us -> none  [on_device(): steps = lax.all_gather(step, everyone, axis=0, tiled=False)]
    all_to_all x1, waiting for transfers between devices: 0.01 us -> 13.7 us  [on_device(): lax.all_to_all(imag.reshape(angles, band // angles, width), 'angle', spli...]
    all_to_all x0 -> x1, starting transfers between devices: none -> 3.55 us  [on_device(): lax.all_to_all(copies, everyone, split_axis=0, concat_axis=0, tiled=True)]
    ppermute x4, waiting for transfers between devices: 19.5 us -> 16.3 us  [passed_along(): return lax.ppermute(array, axis, pairs)]
    all_to_all x1, waiting for transfers between devices: 0.01 us -> 2.71 us  [on_device(): lax.all_to_all(pieces, everyone, split_axis=0, concat_axis=0, tiled=True)]
    ppermute x4, starting transfers between devices: 12.9 us -> 11.8 us  [passed_along(): return lax.ppermute(array, axis, pairs)]
  transfers between devices with their start and end apart: 6 -> 7, of which waited for: 3 -> 5; matrix products, arithmetic and copies ran while one was open for 3% -> 2% of each run, Pallas kernels for 6% -> 8%
where the time goes in v2:
time: 89.2 us; the launch traced here: 88.7 us
  waiting for transfers between devices  32.7 us (37%)
  starting transfers between devices  26.6 us (30%)
  Pallas kernels  20.8 us (23%)
  local copies, waits for them, and re-layouts  6.42 us (7%)
  other arithmetic  1.39 us (2%)
    ppermute x4, waiting for transfers between devices, passed_along(): return lax.ppermute(array, axis, pairs)  16.3 us
    all_to_all x1, waiting for transfers between devices, on_device(): lax.all_to_all(imag.reshape(angles, band // angles, width), 'angle', spli...  13.7 us
    ppermute x4, starting transfers between devices, passed_along(): return lax.ppermute(array, axis, pairs)  11.8 us
    pallas_call x1, Pallas kernels, on_device(): pl.pallas_call(back_kernel, name='back', grid=(width // columns,), out_sh...  7.31 us
    all_to_all x1, starting transfers between devices, on_device(): lax.all_to_all(pieces, everyone, split_axis=0, concat_axis=0, tiled=True)  7.29 us
    pallas_call x1, Pallas kernels, on_device(): pl.pallas_call(gradient_kernel, name='gradient', out_shape=(jax.ShapeDtyp...  6.54 us
    all_to_all x1, starting transfers between devices, on_device(): lax.all_to_all(imag.reshape(angles, band // angles, width), 'angle', spli...  3.99 us
    pallas_call x1, Pallas kernels, on_device(): pl.pallas_call(update_kernel, name='update', out_shape=(jax.ShapeDtypeStr...  3.56 us
  transfers between devices with their start and end apart: 7, of which 5 were waited for; matrix products, arithmetic and copies ran while one was open for 2% of the time, Pallas kernels for 8%

profile of v2, /device:TPU:3, one launch (start us, length us, event | category | flops | bytes accessed | tf_op | source)
XLA Modules:
  0.0 88.7 jit_solution(9063858984516599774)
XLA Ops:
  0.6 0.0 copy-start.6
  0.6 1.3 %fusion = (f32[2,64,1024]{2,1,0:T(8,128)S(1)}, f32[2,64,1024]{2,1,0:T(8,128)S(1)}) fusion(f32[2,128,1024]{2,1,0:T(8,128)} %bitcast.16), kind=kLoop, calls=%fused_computation.4 | loop fusion | bytes 2097152 | tf_op jit(solution)/shard_map/slice | solution.py:202
  1.9 2.6 %collective-permute-start.1 = (f32[2,64,1024]{2,1,0:T(8,128)S(1)}, f32[2,64,1024]{2,1,0:T(8,128)S(1)}, u32[]{:S(2)}, u32[]{:S(2)}) collective-permute-start(f32[2,64,1024]{2,1,0:T(8,128)S(1)} %get-tuple-element.19), channel_id=1, source_target_pairs={{1,0},{2,1},{3,2},{4,3},{5,4},{6,5},{7,6},{9,8},{10,9},{11,10},{12... | collective-permute-start | bytes 1572872 | tf_op jit(solution)/shard_map/ppermute | solution.py:19
  4.5 3.9 %collective-permute-start = (f32[2,64,1024]{2,1,0:T(8,128)S(1)}, f32[2,64,1024]{2,1,0:T(8,128)S(1)}, u32[]{:S(2)}, u32[]{:S(2)}) collective-permute-start(f32[2,64,1024]{2,1,0:T(8,128)S(1)} %get-tuple-element.20), channel_id=1, source_target_pairs={{0,1},{1,2},{2,3},{3,4},{4,5},{5,6},{6,7},{8,9},{9,10},{10,11},{11... | collective-permute-start | bytes 1572872 | tf_op jit(solution)/shard_map/ppermute | solution.py:19
  8.4 0.0 copy-done.6
  8.4 0.1 copy.15
  8.5 3.4 %ramp.1 = (bf16[1024,1024]{1,0:T(8,128)(2,1)}, bf16[1024,1024]{1,0:T(8,128)(2,1)}) custom-call(), custom_call_target="tpu_custom_call" | custom-call | flops 20971520 | bytes 4194304 | tf_op jit(solution)/shard_map/ramp/pallas_call | solution.py:206
  11.9 0.1 pad_add_fusion
  12.0 0.6 broadcast_subtract_fusion.places
  12.6 4.4 %collective-permute-done.1.high_ref = f32[2,64,1024]{2,1,0:T(8,128)S(1)} collective-permute-done((f32[2,64,1024]{2,1,0:T(8,128)S(1)}, f32[2,64,1024]{2,1,0:T(8,128)S(1)}, u32[]{:S(2)}, u32[]{:S(2)}) %collective-permute-start.1) | collective-permute-done | bytes 524320 | tf_op jit(solution)/shard_map/ppermute | solution.py:19
  17.0 0.0 copy-start.3
  17.0 0.0 collective-permute-done.low_ref
  17.0 0.0 copy-start.4
  17.0 0.8 copy-done.3
  17.7 0.2 copy-done.4
  17.9 6.5 %gradient.1 = (f32[3,64,1024]{2,1,0:T(8,128)}, f32[3,128,1024]{2,1,0:T(8,128)}, f32[3,64,1024]{2,1,0:T(8,128)}, f32[128,3,128]{2,1,0:T(4,128)}) custom-call(s32[4,2]{1,0:T(4,128)} %broadcast_subtract_fusion.places, f32[2,64,1024]{2,1,0:T(8,128)} %copy-done.4, f32[2,128,1024]{2,1,0:T(8,128)} %bitcast.17, f32[2,64,1024]{2,1,0:T(8,128)} %copy-done.3, ...), custom_call_target="tpu_custom_call" | custom-call | tf_op jit(solution)/shard_map/gradient/pallas_call | solution.py:214
  24.5 1.7 %copy.16 = f32[32,4,3,128]{3,1,2,0:T(4,128)} copy(f32[32,4,3,128]{3,2,1,0:T(4,128)} %bitcast.23) | data formatting | bytes 393216 | tf_op jit(solution)/shard_map/reshape | solution.py:240
  26.2 7.3 %all-to-all-start = ((f32[32,4,3,128]{3,1,2,0:T(4,128)}), f32[32,4,3,128]{3,1,2,0:T(4,128)S(1)}, u32[]{:S(2)}, u32[]{:S(2)}) async-start(f32[32,4,3,128]{3,1,2,0:T(4,128)} %copy.16), calls=%async_computation | async-start | bytes 393216 | tf_op jit(solution)/shard_map/all_to_all | solution.py:241
  33.5 3.4 %collective-permute-start.2 = (f32[3,64,1024]{2,1,0:T(8,128)}, f32[3,64,1024]{2,1,0:T(8,128)S(1)}, u32[]{:S(2)}, u32[]{:S(2)}) collective-permute-start(f32[3,64,1024]{2,1,0:T(8,128)} %get-tuple-element.13), channel_id=1, source_target_pairs={{0,1},{1,2},{2,3},{3,4},{4,5},{5,6},{6,7},{8,9},{9,10},{10,11},{11... | collective-permute-start | bytes 2359304 | tf_op jit(solution)/shard_map/ppermute | solution.py:19
  36.8 1.9 %collective-permute-start.3 = (f32[3,64,1024]{2,1,0:T(8,128)}, f32[3,64,1024]{2,1,0:T(8,128)S(1)}, u32[]{:S(2)}, u32[]{:S(2)}) collective-permute-start(f32[3,64,1024]{2,1,0:T(8,128)} %get-tuple-element.14), channel_id=1, source_target_pairs={{1,0},{2,1},{3,2},{4,3},{5,4},{6,5},{7,6},{9,8},{10,9},{11,10},{12... | collective-permute-start | bytes 2359304 | tf_op jit(solution)/shard_map/ppermute | solution.py:19
  38.8 2.7 %all-to-all-done = f32[32,4,3,128]{3,1,2,0:T(4,128)S(1)} async-done(((f32[32,4,3,128]{3,1,2,0:T(4,128)}), f32[32,4,3,128]{3,1,2,0:T(4,128)S(1)}, u32[]{:S(2)}, u32[]{:S(2)}) %all-to-all-start) | async-done | bytes 196640 | tf_op jit(solution)/shard_map/all_to_all | solution.py:241
  41.5 0.1 reduce_sum.9
  41.6 0.7 broadcast_in_dim.14
  42.3 3.5 %all-to-all-start.1 = ((f32[32,4,2,128]{3,1,2,0:T(4,128)}), f32[32,4,2,128]{3,1,2,0:T(4,128)S(1)}, u32[]{:S(2)}, u32[]{:S(2)}) async-start(f32[32,4,2,128]{3,1,2,0:T(4,128)} %broadcast_in_dim.14), calls=%async_computation.1 | async-start | bytes 262144 | tf_op jit(solution)/shard_map/all_to_all | solution.py:244
  45.8 8.0 %collective-permute-done.2.above_ref = f32[3,64,1024]{2,1,0:T(8,128)S(1)} collective-permute-done((f32[3,64,1024]{2,1,0:T(8,128)}, f32[3,64,1024]{2,1,0:T(8,128)S(1)}, u32[]{:S(2)}, u32[]{:S(2)}) %collective-permute-start.2) | collective-permute-done | bytes 786464 | tf_op jit(solution)/shard_map/ppermute | solution.py:19
  53.8 0.0 copy-start.1
  53.8 3.9 %collective-permute-done.3.below_ref = f32[3,64,1024]{2,1,0:T(8,128)S(1)} collective-permute-done((f32[3,64,1024]{2,1,0:T(8,128)}, f32[3,64,1024]{2,1,0:T(8,128)S(1)}, u32[]{:S(2)}, u32[]{:S(2)}) %collective-permute-start.3) | collective-permute-done | bytes 786464 | tf_op jit(solution)/shard_map/ppermute | solution.py:19
  57.7 0.0 copy-start.2
  57.7 0.0 copy-done.1
  57.7 0.9 copy-done.2
  58.6 0.0 copy-start.5
  58.6 3.6 %update.1 = (f32[2,128,1024]{2,1,0:T(8,128)}, f32[128,1024]{1,0:T(8,128)}) custom-call(f32[2,128,1024]{2,1,0:T(8,128)} %bitcast.18, f32[3,128,1024]{2,1,0:T(8,128)} %get-tuple-element.12.own_ref, f32[3,64,1024]{2,1,0:T(8,128)} %copy-done.1, f32[3,64,1024]{2,1,0:T(8,128)} %copy-done.2), custom_call_target="tpu_custom_call" | custom-call | tf_op jit(solution)/shard_map/update/pallas_call | solution.py:229
  62.2 0.0 all-to-all-done.1
  62.2 4.0 %all-to-all-start.2 = ((f32[4,32,1024]{2,1,0:T(8,128)}), f32[4,32,1024]{2,1,0:T(8,128)S(1)}, u32[]{:S(2)}, u32[]{:S(2)}) async-start(f32[4,32,1024]{2,1,0:T(8,128)} %bitcast.20), calls=%async_computation.2 | async-start | bytes 1048576 | tf_op jit(solution)/shard_map/all_to_all | solution.py:239
  66.2 0.0 copy-done.5
  66.2 0.7 add.12
  66.9 13.7 %all-to-all-done.2.sino_ref = f32[4,32,1024]{2,1,0:T(8,128)S(1)} async-done(((f32[4,32,1024]{2,1,0:T(8,128)}), f32[4,32,1024]{2,1,0:T(8,128)S(1)}, u32[]{:S(2)}, u32[]{:S(2)}) %all-to-all-start.2) | async-done | bytes 524320 | tf_op jit(solution)/shard_map/all_to_all | solution.py:239
  80.6 0.0 copy-start
  80.6 0.8 copy-done
  81.4 7.3 %back.1 = f32[32,2,1024]{2,1,0:T(2,128)} custom-call(f32[4,32,1024]{2,1,0:T(8,128)} %copy-done, bf16[1024,1024]{1,0:T(8,128)(2,1)} %get-tuple-element.11.ramp_ref.ramp_high_ref, bf16[1024,1024]{1,0:T(8,128)(2,1)} %get-tuple-element.18.ramp_low_ref, s32[4,2,1024]{2,1,0:T(2,128)} %index_ref.1, f32[4,2,1024]{2,1,0:T(2,128)} %weight_ref.1), custom_call_target="tpu_custom_call" | custom-call | tf_op jit(solution)/shard_map/back/pallas_call | solution.py:249
  (5 shorter events, 0.0 us)
Async XLA Ops:
  0.6 7.8 %copy-start.6 = (s32[1,4,2]{1,2,0:T(2,128)S(1)}, s32[1,4,2]{1,2,0:T(2,128)}, u32[]{:S(2)}) copy-start(s32[1,4,2]{1,2,0:T(2,128)} %param.8) | copy-start | bytes 100
  1.9 15.0 %collective-permute-start.1 = (f32[2,64,1024]{2,1,0:T(8,128)S(1)}, f32[2,64,1024]{2,1,0:T(8,128)S(1)}, u32[]{:S(2)}, u32[]{:S(2)}) collective-permute-start(f32[2,64,1024]{2,1,0:T(8,128)S(1)} %get-tuple-element.19), channel_id=1, source_target_pairs={{1,0},{2,1},{3,2},{4,3},{5,4},{6,5},{7,6},{9,8},{10,9},{11,10},{12... | collective-permute-start | bytes 1572872 | tf_op jit(solution)/shard_map/ppermute | solution.py:19
  4.5 12.5 %collective-permute-start = (f32[2,64,1024]{2,1,0:T(8,128)S(1)}, f32[2,64,1024]{2,1,0:T(8,128)S(1)}, u32[]{:S(2)}, u32[]{:S(2)}) collective-permute-start(f32[2,64,1024]{2,1,0:T(8,128)S(1)} %get-tuple-element.20), channel_id=1, source_target_pairs={{0,1},{1,2},{2,3},{3,4},{4,5},{5,6},{6,7},{8,9},{9,10},{10,11},{11... | collective-permute-start | bytes 1572872 | tf_op jit(solution)/shard_map/ppermute | solution.py:19
  17.0 0.8 copy-start.3
  17.0 1.0 %copy-start.4 = (f32[2,64,1024]{2,1,0:T(8,128)}, f32[2,64,1024]{2,1,0:T(8,128)S(1)}, u32[]{:S(2)}) copy-start(f32[2,64,1024]{2,1,0:T(8,128)S(1)} %collective-permute-done.low_ref) | copy-start | bytes 1572868
  26.2 15.3 %all-to-all-start = ((f32[32,4,3,128]{3,1,2,0:T(4,128)}), f32[32,4,3,128]{3,1,2,0:T(4,128)S(1)}, u32[]{:S(2)}, u32[]{:S(2)}) async-start(f32[32,4,3,128]{3,1,2,0:T(4,128)} %copy.16), calls=%async_computation | async-start | bytes 393216 | tf_op jit(solution)/shard_map/all_to_all | solution.py:241
  33.5 20.4 %collective-permute-start.2 = (f32[3,64,1024]{2,1,0:T(8,128)}, f32[3,64,1024]{2,1,0:T(8,128)S(1)}, u32[]{:S(2)}, u32[]{:S(2)}) collective-permute-start(f32[3,64,1024]{2,1,0:T(8,128)} %get-tuple-element.13), channel_id=1, source_target_pairs={{0,1},{1,2},{2,3},{3,4},{4,5},{5,6},{6,7},{8,9},{9,10},{10,11},{11... | collective-permute-start | bytes 2359304 | tf_op jit(solution)/shard_map/ppermute | solution.py:19
  36.8 20.9 %collective-permute-start.3 = (f32[3,64,1024]{2,1,0:T(8,128)}, f32[3,64,1024]{2,1,0:T(8,128)S(1)}, u32[]{:S(2)}, u32[]{:S(2)}) collective-permute-start(f32[3,64,1024]{2,1,0:T(8,128)} %get-tuple-element.14), channel_id=1, source_target_pairs={{1,0},{2,1},{3,2},{4,3},{5,4},{6,5},{7,6},{9,8},{10,9},{11,10},{12... | collective-permute-start | bytes 2359304 | tf_op jit(solution)/shard_map/ppermute | solution.py:19
  42.3 19.9 %all-to-all-start.1 = ((f32[32,4,2,128]{3,1,2,0:T(4,128)}), f32[32,4,2,128]{3,1,2,0:T(4,128)S(1)}, u32[]{:S(2)}, u32[]{:S(2)}) async-start(f32[32,4,2,128]{3,1,2,0:T(4,128)} %broadcast_in_dim.14), calls=%async_computation.1 | async-start | bytes 262144 | tf_op jit(solution)/shard_map/all_to_all | solution.py:244
  53.8 3.9 %copy-start.1 = (f32[3,64,1024]{2,1,0:T(8,128)}, f32[3,64,1024]{2,1,0:T(8,128)S(1)}, u32[]{:S(2)}) copy-start(f32[3,64,1024]{2,1,0:T(8,128)S(1)} %collective-permute-done.2.above_ref) | copy-start | bytes 2359300
  57.7 0.9 copy-start.2
  58.6 7.6 %copy-start.5 = (f32[2,128,128]{2,1,0:T(8,128)S(1)}, f32[2,128,128]{2,1,0:T(8,128)}, u32[]{:S(2)}) copy-start(f32[2,128,128]{2,1,0:T(8,128)} %probe_ref.1) | copy-start | bytes 393220
  62.2 18.4 %all-to-all-start.2 = ((f32[4,32,1024]{2,1,0:T(8,128)}), f32[4,32,1024]{2,1,0:T(8,128)S(1)}, u32[]{:S(2)}, u32[]{:S(2)}) async-start(f32[4,32,1024]{2,1,0:T(8,128)} %bitcast.20), calls=%async_computation.2 | async-start | bytes 1048576 | tf_op jit(solution)/shard_map/all_to_all | solution.py:239
  80.6 0.8 copy-start

commit v3 on v2

--- a/solution.py
+++ b/solution.py
@@ -7,6 +7,7 @@
 from jax.experimental import pallas as pl
 from jax.experimental.pallas import tpu as pltpu
 from jax.sharding import PartitionSpec as P
+
 
 LANES = 128
 ROWS = 8
@@ -48,17 +49,80 @@
     return dot(left_high, right_high) + (dot(left_high, right_low) + dot(left_low, right_high))
 
 
+def row_spot(row):
+    top = pl.multiple_of(row // ROWS * ROWS, ROWS)
+    return top, row - top
+
+
+def column_spot(col, last):
+    base = pl.multiple_of(jnp.minimum(col // LANES, last) * LANES, LANES)
+    return base, col - base
+
+
+def spread_rows(column, term, top, drop):
+    tall = term.shape[0] + ROWS
+    column[...] = jnp.zeros(column.shape, jnp.float32)
+    blank = jnp.zeros((ROWS, term.shape[1]), jnp.float32)
+    column[pl.ds(top, tall)] = pltpu.roll(jnp.concatenate([term, blank], axis=0), drop, 0)
+
+
+def add_columns(ref, lead, term, base, shift):
+    blank = jnp.zeros((term.shape[0], LANES), jnp.float32)
+    wide = pltpu.roll(jnp.concatenate([term, blank], axis=1), shift, 1)
+    spot = lead + (pl.ds(base, term.shape[1] + LANES),)
+    ref[spot] = ref[spot] + wide
+
+
+def pack_kernel(places, block_ref, up_ref, down_ref):
+    band, width = block_ref.shape[1], block_ref.shape[2]
+    half = (up_ref.shape[0] - ROWS) // 2
+    lane = lax.broadcasted_iota(jnp.int32, (ROWS, width), 1)
+    note = jnp.zeros((ROWS, width), jnp.int32)
+    for b in range(places.shape[0]):
+        for i in range(2):
+            note = jnp.where(lane == 2 * b + i, places[b, i] + 1, note)
+    note = note.astype(jnp.float32)
+    for ch in range(2):
+        up_ref[ch * half:(ch + 1) * half] = block_ref[ch, :half]
+        down_ref[ch * half:(ch + 1) * half] = block_ref[ch, band - half:]
+    up_ref[2 * half:] = note
+    down_ref[2 * half:] = note
+
+
+def weight_kernel(near, probe_ref, out_ref, total, column):
+    band, width = out_ref.shape
+    patch = probe_ref.shape[1]
+    half = patch // 2
+    last = width // LANES - patch // LANES - 1
+    power = probe_ref[0] * probe_ref[0] + probe_ref[1] * probe_ref[1]
+    total[...] = jnp.ones(total.shape, jnp.float32)
+    for b in range(near.shape[0]):
+        group = b * 3 // near.shape[0]
+        top, drop = row_spot(near[b, 0])
+        base, shift = column_spot(near[b, 1], last)
+        term = power * near[b, 2].astype(jnp.float32)
+        slot = column.at[b % 2]
+        spread_rows(slot, term, top, drop)
+        if group == 0:
+            add_columns(total, (slice(None),), slot[half:half + band], base, shift)
+        elif group == 1:
+            add_columns(total, (slice(0, half),), slot[half + band:], base, shift)
+        else:
+            add_columns(total, (slice(band - half, band),), slot[:half], base, shift)
+    out_ref[...] = 1.0 / total[...]
+
+
 def gradient_kernel(places, low_ref, block_ref, high_ref, probe_ref, amp_ref, table_ref, ramp_ref,
-                    up_ref, own_ref, down_ref, stat_ref, field, total):
+                    up_ref, own_ref, down_ref, stat_ref, field, column):
     count, patch = amp_ref.shape[0], amp_ref.shape[1]
-    half, band, width = low_ref.shape[1], block_ref.shape[1], block_ref.shape[2]
-    field[:, :half] = low_ref[...]
+    half, band, width = patch // 2, block_ref.shape[1], block_ref.shape[2]
     field[:, half:half + band] = block_ref[...]
-    field[:, half + band:] = high_ref[...]
-    total[...] = jnp.zeros(total.shape, jnp.float32)
+    for ch in range(2):
+        field[ch, :half] = low_ref[ch * half:(ch + 1) * half]
+        field[ch, half + band:] = high_ref[ch * half:(ch + 1) * half]
+    own_ref[...] = jnp.zeros(own_ref.shape, jnp.float32)
     probe_real = probe_ref[0]
     probe_imag = probe_ref[1]
-    power = probe_real * probe_real + probe_imag * probe_imag
     window = patch + LANES
     tall = patch + ROWS
     last = (width - window) // LANES
@@ -68,10 +132,8 @@
     for b in range(count):
         row = places[b, 0]
         col = places[b, 1]
-        top = pl.multiple_of(row // ROWS * ROWS, ROWS)
-        base = pl.multiple_of(jnp.minimum(col // LANES, last) * LANES, LANES)
-        drop = row - top
-        shift = col - base
+        top, drop = row_spot(row)
+        base, shift = column_spot(col, last)
         spots.append((top, drop, base, shift))
         cut = []
         for ch in range(2):
@@ -107,8 +169,6 @@
     numer_real = jnp.zeros((patch, patch), jnp.float32)
     numer_imag = jnp.zeros((patch, patch), jnp.float32)
     denom = jnp.zeros((patch, patch), jnp.float32)
-    blank = jnp.zeros((tall, LANES), jnp.float32)
-    blank_rows = jnp.zeros((ROWS, patch), jnp.float32)
     for b in range(count):
         top, drop, base, shift = spots[b]
         cut_real, cut_imag = patches[b]
@@ -118,36 +178,32 @@
         numer_imag += cut_real * diff_imag - cut_imag * diff_real
         denom += cut_real * cut_real + cut_imag * cut_imag
         terms = (probe_real * diff_real + probe_imag * diff_imag,
-                 probe_real * diff_imag - probe_imag * diff_real, power)
+                 probe_real * diff_imag - probe_imag * diff_real)
         for ch, term in enumerate(terms):
-            tall_term = pltpu.roll(jnp.concatenate([term, blank_rows], axis=0), drop, 0)
-            wide = pltpu.roll(jnp.concatenate([tall_term, blank], axis=1), shift, 1)
-            spot = (ch, pl.ds(top, tall), pl.ds(base, window))
-            total[spot] = total[spot] + wide
+            spread_rows(column.at[ch], term, top, drop)
+            up_ref[ch, b] = column[ch, :half]
+            add_columns(own_ref, (ch, slice(None)), column[ch, half:half + band], base, shift)
+            down_ref[ch, b] = column[ch, half + band:]
     stat_ref[:, 0, :] = numer_real
     stat_ref[:, 1, :] = numer_imag
     stat_ref[:, 2, :] = denom
-    up_ref[...] = total[:, :half]
-    own_ref[...] = total[:, half:half + band]
-    down_ref[...] = total[:, half + band:]
-
-
-def update_kernel(object_ref, own_ref, above_ref, below_ref, out_ref, imag_ref):
-    band = own_ref.shape[1]
-    half = above_ref.shape[1]
-    ends = sorted({0, half, band - half, band})
-    for start, stop in zip(ends[:-1], ends[1:]):
-        terms = [own_ref[ch, start:stop] for ch in range(3)]
-        if stop <= half:
-            terms = [terms[ch] + above_ref[ch, start:stop] for ch in range(3)]
-        if start >= band - half:
-            offset = band - half
-            terms = [terms[ch] + below_ref[ch, start - offset:stop - offset] for ch in range(3)]
-        scale = terms[2] + 1.0
-        out_ref[0, start:stop] = object_ref[0, start:stop] + terms[0] / scale
-        imag = object_ref[1, start:stop] + terms[1] / scale
-        out_ref[1, start:stop] = imag
-        imag_ref[start:stop] = imag
+
+
+def update_kernel(near, object_ref, own_ref, weight_ref, above_ref, below_ref, out_ref, imag_ref, total):
+    band, width = own_ref.shape[1], own_ref.shape[2]
+    count, half, patch = above_ref.shape[1], above_ref.shape[2], above_ref.shape[3]
+    last = width // LANES - patch // LANES - 1
+    total[...] = own_ref[...]
+    for b in range(count):
+        for group, ref, start in ((1, above_ref, 0), (2, below_ref, band - half)):
+            base, shift = column_spot(near[group * count + b, 1], last)
+            for ch in range(2):
+                add_columns(total, (ch, slice(start, start + half)), ref[ch, b], base, shift)
+    scale = weight_ref[...]
+    out_ref[0] = object_ref[0] + total[0] * scale
+    imag = object_ref[1] + total[1] * scale
+    out_ref[1] = imag
+    imag_ref[...] = imag
 
 
 def ramp_kernel(high_ref, low_ref):
@@ -198,10 +254,26 @@
     vmem = pl.BlockSpec(memory_space=pltpu.VMEM)
     smem = pl.BlockSpec(memory_space=pltpu.SMEM)
     layer = object_field[0]
-    low = passed_along(layer[:, band - half:], "pos", 1)
-    high = passed_along(layer[:, :half], "pos", -1)
+    count = offsets.shape[1]
+    packed = jax.ShapeDtypeStruct((2 * half + ROWS, width), f32)
+    to_above, to_below = pl.pallas_call(
+        pack_kernel,
+        name="pack",
+        out_shape=(packed, packed),
+        in_specs=[smem, vmem],
+        out_specs=[vmem] * 2,
+    )(offsets[0], layer)
+    low = passed_along(to_below, "pos", 1)
+    high = passed_along(to_above, "pos", -1)
     anchor = lax.axis_index("pos") * band - half
     places = offsets[0] - jnp.stack([anchor, 0]).astype(jnp.int32)
+    near = [jnp.concatenate([places, jnp.ones((count, 1), jnp.int32)], axis=1)]
+    for message, far in ((low, anchor - band), (high, anchor + band)):
+        note = message[2 * half, :2 * count].reshape(count, 2).astype(jnp.int32)
+        valid = note[:, 1:] > 0
+        there = note - 1 - jnp.stack([far, 0]).astype(jnp.int32)
+        near.append(jnp.concatenate([jnp.where(valid, there, 0), valid.astype(jnp.int32)], axis=1))
+    near = jnp.concatenate(near, axis=0)
     ramp_rows = width // 4
     ramp_high, ramp_low = pl.pallas_call(
         ramp_kernel,
@@ -215,32 +287,44 @@
         gradient_kernel,
         name="gradient",
         out_shape=(
-            jax.ShapeDtypeStruct((3, half, width), f32),
-            jax.ShapeDtypeStruct((3, band, width), f32),
-            jax.ShapeDtypeStruct((3, half, width), f32),
+            jax.ShapeDtypeStruct((2, count, half, patch), f32),
+            jax.ShapeDtypeStruct((2, band, width), f32),
+            jax.ShapeDtypeStruct((2, count, half, patch), f32),
             jax.ShapeDtypeStruct((patch, 3, patch), f32),
         ),
         in_specs=[smem] + [vmem] * 6 + [pl.BlockSpec(memory_space=pl.ANY)],
         out_specs=[vmem] * 4,
-        scratch_shapes=[pltpu.VMEM((2, band + patch, width), f32), pltpu.VMEM((3, band + patch, width), f32)],
+        scratch_shapes=[pltpu.VMEM((2, band + patch, width), f32), pltpu.VMEM((2, band + patch, patch), f32)],
     )(places, low, layer, high, probe_field, amplitude[0], dft_tables(patch), ramp_high)
     from_below = passed_along(up, "pos", -1)
     from_above = passed_along(down, "pos", 1)
+    weight = pl.pallas_call(
+        weight_kernel,
+        name="weight",
+        out_shape=jax.ShapeDtypeStruct((band, width), f32),
+        in_specs=[smem, vmem],
+        out_specs=vmem,
+        scratch_shapes=[pltpu.VMEM((band, width), f32), pltpu.VMEM((2, band + patch, patch), f32)],
+        cost_estimate=pl.CostEstimate(flops=20 * width * width, transcendentals=0, bytes_accessed=4 * band * width),
+    )(near, probe_field)
     new_layer, imag = pl.pallas_call(
         update_kernel,
         name="update",
         out_shape=(jax.ShapeDtypeStruct((2, band, width), f32), jax.ShapeDtypeStruct((band, width), f32)),
-        in_specs=[vmem] * 4,
+        in_specs=[smem] + [vmem] * 5,
         out_specs=[vmem] * 2,
-    )(layer, own, from_above, from_below)
+        scratch_shapes=[pltpu.VMEM((2, band, width), f32)],
+    )(near, layer, own, weight, from_above, from_below)
     everyone = ("angle", "pos")
     shares = lax.axis_size("angle") * lax.axis_size("pos")
     angles = lax.axis_size("angle")
     regrouped = lax.all_to_all(imag.reshape(angles, band // angles, width), "angle", split_axis=0, concat_axis=0, tiled=True)
     pieces = stats.reshape(shares, patch // shares, 3, patch)
-    mine = jnp.sum(lax.all_to_all(pieces, everyone, split_axis=0, concat_axis=0, tiled=True), axis=0)
+    shared = lax.all_to_all(pieces, everyone, split_axis=0, concat_axis=0, tiled=True)
+    mine = jnp.sum(shared, axis=0)
     step = mine[:, :2] / (mine[:, 2:] + 1.0)
     copies = jnp.broadcast_to(step[None], (shares,) + step.shape)
+    copies, regrouped = lax.optimization_barrier((copies, regrouped))
     steps = lax.all_to_all(copies, everyone, split_axis=0, concat_axis=0, tiled=True)
     new_probe = probe_field + jnp.swapaxes(steps.reshape(patch, 2, patch), 0, 1)
     rows = band // angles
@@ -274,6 +358,7 @@
         P(),
         P(),
     )
+
     return jax.shard_map(
         on_device,
         mesh=mesh,

time: 89.2 us -> 84.1 us (0.943)
  the two profiles are of different devices: /device:TPU:3 before, /device:TPU:0 now
where the time goes in v3:
time: 84.1 us; the launch traced here: 83.6 us
  starting transfers between devices  36.6 us (44%)
  Pallas kernels  24.4 us (29%)
  waiting for transfers between devices  13.1 us (16%)
  local copies, waits for them, and re-layouts  5.45 us (6%)
  other arithmetic  3.25 us (4%)
    all_to_all x1, starting transfers between devices, on_device(): lax.all_to_all(pieces, everyone, split_axis=0, concat_axis=0, tiled=True)  15 us
    all_to_all x1, waiting for transfers between devices, on_device(): lax.all_to_all(imag.reshape(angles, band // angles, width), 'angle', spli...  12.2 us
    all_to_all x1, starting transfers between devices, on_device(): lax.all_to_all(copies, everyone, split_axis=0, concat_axis=0, tiled=True)  9.68 us
    pallas_call x1, Pallas kernels, on_device(): pl.pallas_call(back_kernel, name='back', grid=(width // columns,), out_sh...  7.36 us
    ppermute x4, starting transfers between devices, passed_along(): return lax.ppermute(array, axis, pairs)  7.17 us
    pallas_call x1, Pallas kernels, on_device(): pl.pallas_call(gradient_kernel, name='gradient', out_shape=(jax.ShapeDtyp...  5.62 us
    all_to_all x1, starting transfers between devices, on_device(): lax.all_to_all(imag.reshape(angles, band // angles, width), 'angle', spli...  4.76 us
    pallas_call x1, Pallas kernels, on_device(): pl.pallas_call(ramp_kernel, name='ramp', grid=(width // ramp_rows,), out_...  3.42 us
  transfers between devices with their start and end apart: 7, of which 3 were waited for; matrix products, arithmetic and copies ran while one was open for 3% of the time, Pallas kernels for 20%

profile of v3, /device:TPU:0, one launch (start us, length us, event | category | flops | bytes accessed | tf_op | source)
XLA Modules:
  0.0 83.6 jit_solution(11417989756550277627)
XLA Ops:
  0.6 1.3 %copy.35.places = s32[4,2]{1,0:T(4,128)} copy(s32[4,2]{0,1:T(2,128)} %bitcast.26) | data formatting | bytes 64 | tf_op jit(solution)/shard_map/squeeze | solution.py:269
  2.0 2.3 %pack.1 = (f32[136,1024]{1,0:T(8,128)}, f32[136,1024]{1,0:T(8,128)}) custom-call(s32[4,2]{1,0:T(4,128)} %copy.35.places, f32[2,128,1024]{2,1,0:T(8,128)} %bitcast.18), custom_call_target="tpu_custom_call" | custom-call | tf_op jit(solution)/shard_map/pack/pallas_call | solution.py:259
  4.3 2.4 %collective-permute-start = (f32[136,1024]{1,0:T(8,128)}, f32[136,1024]{1,0:T(8,128)S(1)}, u32[]{:S(2)}, u32[]{:S(2)}) collective-permute-start(f32[136,1024]{1,0:T(8,128)} %get-tuple-element.15), channel_id=1, source_target_pairs={{0,1},{1,2},{2,3},{3,4},{4,5},{5,6},{6,7},{8,9},{9,10},{10,11},{11... | collective-permute-start | bytes 1671176 | tf_op jit(solution)/shard_map/ppermute | solution.py:20
  6.7 1.3 %collective-permute-start.1 = (f32[136,1024]{1,0:T(8,128)}, f32[136,1024]{1,0:T(8,128)S(1)}, u32[]{:S(2)}, u32[]{:S(2)}) collective-permute-start(f32[136,1024]{1,0:T(8,128)} %get-tuple-element.16), channel_id=1, source_target_pairs={{1,0},{2,1},{3,2},{4,3},{5,4},{6,5},{7,6},{9,8},{10,9},{11,10},{12... | collective-permute-start | bytes 1671176 | tf_op jit(solution)/shard_map/ppermute | solution.py:20
  8.0 3.4 %ramp.1 = (bf16[1024,1024]{1,0:T(8,128)(2,1)}, bf16[1024,1024]{1,0:T(8,128)(2,1)}) custom-call(), custom_call_target="tpu_custom_call" | custom-call | flops 20971520 | bytes 4194304 | tf_op jit(solution)/shard_map/ramp/pallas_call | solution.py:278
  11.4 0.1 pad_add_fusion.2
  11.5 0.1 pad_add_fusion
  11.6 1.3 %broadcast_subtract_fusion.places = s32[4,2]{1,0:T(4,128)} fusion(s32[4,2]{1,0:T(4,128)} %copy.35.places, s32[2]{0:T(128)S(1)} %pad_add_fusion.2), kind=kLoop, calls=%fused_computation.9 | loop fusion | flops 8 | bytes 72 | tf_op jit(solution)/shard_map/sub | solution.py:269
  12.8 0.0 collective-permute-done.low_ref
  12.8 0.0 copy-start.2
  12.8 0.1 convert_element_type.19
  12.9 0.0 collective-permute-done.1.high_ref
  12.9 0.0 copy-start.3
  12.9 0.1 convert_element_type.22
  13.0 0.6 copy-done.2
  13.7 0.1 copy-done.3
  13.8 0.0 copy-start.6
  13.8 5.6 %gradient.1 = (f32[2,4,64,128]{3,2,1,0:T(8,128)}, f32[2,128,1024]{2,1,0:T(8,128)}, f32[2,4,64,128]{3,2,1,0:T(8,128)}, f32[128,3,128]{2,1,0:T(4,128)}) custom-call(s32[4,2]{1,0:T(4,128)} %broadcast_subtract_fusion.places, f32[136,1024]{1,0:T(8,128)} %copy-done.2, f32[2,128,1024]{2,1,0:T(8,128)} %bitcast.19, f32[136,1024]{1,0:T(8,128)} %copy-done.3, ...), custom_call_target="tpu_custom_call" | custom-call | tf_op jit(solution)/shard_map/gradient/pallas_call | solution.py:286
  19.4 1.7 %copy.37 = f32[32,4,3,128]{3,1,2,0:T(4,128)} copy(f32[32,4,3,128]{3,2,1,0:T(4,128)} %bitcast.25) | data formatting | bytes 393216 | tf_op jit(solution)/shard_map/reshape | solution.py:322
  21.1 15.0 %all-to-all-start = ((f32[32,4,3,128]{3,1,2,0:T(4,128)}), f32[32,4,3,128]{3,1,2,0:T(4,128)S(1)}, u32[]{:S(2)}, u32[]{:S(2)}) async-start(f32[32,4,3,128]{3,1,2,0:T(4,128)} %copy.37), calls=%async_computation | async-start | bytes 393216 | tf_op jit(solution)/shard_map/all_to_all | solution.py:323
  36.1 2.2 %collective-permute-start.2 = (f32[2,4,64,128]{3,2,1,0:T(8,128)}, f32[2,4,64,128]{3,2,1,0:T(8,128)S(1)}, u32[]{:S(2)}, u32[]{:S(2)}) collective-permute-start(f32[2,4,64,128]{3,2,1,0:T(8,128)} %get-tuple-element.19), channel_id=1, source_target_pairs={{0,1},{1,2},{2,3},{3,4},{4,5},{5,6},{6,7},{8,9},{9,10},{10,11},{11... | collective-permute-start | bytes 786440 | tf_op jit(solution)/shard_map/ppermute | solution.py:20
  38.3 1.3 %collective-permute-start.3 = (f32[2,4,64,128]{3,2,1,0:T(8,128)}, f32[2,4,64,128]{3,2,1,0:T(8,128)S(1)}, u32[]{:S(2)}, u32[]{:S(2)}) collective-permute-start(f32[2,4,64,128]{3,2,1,0:T(8,128)} %get-tuple-element.20), channel_id=1, source_target_pairs={{1,0},{2,1},{3,2},{4,3},{5,4},{6,5},{7,6},{9,8},{10,9},{11,10},{12... | collective-permute-start | bytes 786440 | tf_op jit(solution)/shard_map/ppermute | solution.py:20
  39.6 0.2 fusion.3
  39.8 0.1 subtract_select_fusion
  39.9 0.1 subtract_select_fusion.1
  40.0 0.0 copy-done.6
  40.0 0.7 fusion.near
  40.7 2.3 %weight.1.weight_ref = f32[128,1024]{1,0:T(8,128)} custom-call(s32[12,3]{1,0:T(8,128)} %fusion.near, f32[2,128,128]{2,1,0:T(8,128)} %probe_ref.3), custom_call_target="tpu_custom_call" | custom-call | flops 20971520 | bytes 524288 | tf_op jit(solution)/shard_map/weight/pallas_call | solution.py:301
  43.0 0.0 collective-permute-done.2.above_ref
  43.0 0.0 copy-start.4
  43.0 0.1 collective-permute-done.3.below_ref
  43.1 0.0 copy-start.5
  43.1 0.6 copy-done.4
  43.7 0.1 copy-done.5
  43.8 3.4 %update.1 = (f32[2,128,1024]{2,1,0:T(8,128)}, f32[128,1024]{1,0:T(8,128)}) custom-call(s32[12,3]{1,0:T(8,128)} %fusion.near, f32[2,128,1024]{2,1,0:T(8,128)} %bitcast.20, f32[2,128,1024]{2,1,0:T(8,128)} %get-tuple-element.18.own_ref, f32[128,1024]{1,0:T(8,128)} %weight.1.weight_ref, f32[2,4,64,128]{3,2,1,0:T(8,128)} %copy-done.4, f32[2,4,64,128]{3,2,1,0:T(8,128)} %copy-done.5), custom_call_target="tpu_custom_call" | custom-call | tf_op jit(solution)/shard_map/update/pallas_call | solution.py:310
  47.2 0.0 all-to-all-done
  47.2 4.8 %all-to-all-start.1 = ((f32[4,32,1024]{2,1,0:T(8,128)}), f32[4,32,1024]{2,1,0:T(8,128)S(1)}, u32[]{:S(2)}, u32[]{:S(2)}) async-start(f32[4,32,1024]{2,1,0:T(8,128)} %bitcast.22), calls=%async_computation.1 | async-start | bytes 1048576 | tf_op jit(solution)/shard_map/all_to_all | solution.py:321
  52.0 0.1 reduce_sum.9
  52.1 12.2 %all-to-all-done.1.sino_ref = f32[4,32,1024]{2,1,0:T(8,128)S(1)} async-done(((f32[4,32,1024]{2,1,0:T(8,128)}), f32[4,32,1024]{2,1,0:T(8,128)S(1)}, u32[]{:S(2)}, u32[]{:S(2)}) %all-to-all-start.1) | async-done | bytes 524320 | tf_op jit(solution)/shard_map/all_to_all | solution.py:321
  64.3 0.0 copy-start
  64.3 0.7 broadcast_in_dim.43
  65.0 9.7 %all-to-all-start.2 = ((f32[32,4,2,128]{3,1,2,0:T(4,128)}), f32[32,4,2,128]{3,1,2,0:T(4,128)S(1)}, u32[]{:S(2)}, u32[]{:S(2)}) async-start(f32[32,4,2,128]{3,1,2,0:T(4,128)} %broadcast_in_dim.43), calls=%async_computation.2 | async-start | bytes 262144 | tf_op jit(solution)/shard_map/all_to_all | solution.py:328
  74.7 0.0 copy-done
  74.7 0.0 copy-start.1
  74.7 7.4 %back.1 = f32[32,2,1024]{2,1,0:T(2,128)} custom-call(f32[4,32,1024]{2,1,0:T(8,128)} %copy-done, bf16[1024,1024]{1,0:T(8,128)(2,1)} %get-tuple-element.17.ramp_ref.ramp_high_ref, bf16[1024,1024]{1,0:T(8,128)(2,1)} %get-tuple-element.26.ramp_low_ref, s32[4,2,1024]{2,1,0:T(2,128)} %index_ref.1, f32[4,2,1024]{2,1,0:T(2,128)} %weight_ref.1), custom_call_target="tpu_custom_call" | custom-call | tf_op jit(solution)/shard_map/back/pallas_call | solution.py:333
  82.1 0.8 all-to-all-done.2
  82.9 0.0 copy-done.1
  82.9 0.7 add.25
  (9 shorter events, 0.1 us)
Async XLA Ops:
  4.3 8.6 %collective-permute-start = (f32[136,1024]{1,0:T(8,128)}, f32[136,1024]{1,0:T(8,128)S(1)}, u32[]{:S(2)}, u32[]{:S(2)}) collective-permute-start(f32[136,1024]{1,0:T(8,128)} %get-tuple-element.15), channel_id=1, source_target_pairs={{0,1},{1,2},{2,3},{3,4},{4,5},{5,6},{6,7},{8,9},{9,10},{10,11},{11... | collective-permute-start | bytes 1671176 | tf_op jit(solution)/shard_map/ppermute | solution.py:20
  6.7 6.2 %collective-permute-start.1 = (f32[136,1024]{1,0:T(8,128)}, f32[136,1024]{1,0:T(8,128)S(1)}, u32[]{:S(2)}, u32[]{:S(2)}) collective-permute-start(f32[136,1024]{1,0:T(8,128)} %get-tuple-element.16), channel_id=1, source_target_pairs={{1,0},{2,1},{3,2},{4,3},{5,4},{6,5},{7,6},{9,8},{10,9},{11,10},{12... | collective-permute-start | bytes 1671176 | tf_op jit(solution)/shard_map/ppermute | solution.py:20
  12.8 0.8 %copy-start.2 = (f32[136,1024]{1,0:T(8,128)}, f32[136,1024]{1,0:T(8,128)S(1)}, u32[]{:S(2)}) copy-start(f32[136,1024]{1,0:T(8,128)S(1)} %collective-permute-done.low_ref) | copy-start | bytes 1671172
  12.9 0.9 %copy-start.3 = (f32[136,1024]{1,0:T(8,128)}, f32[136,1024]{1,0:T(8,128)S(1)}, u32[]{:S(2)}) copy-start(f32[136,1024]{1,0:T(8,128)S(1)} %collective-permute-done.1.high_ref) | copy-start | bytes 1671172
  13.8 26.2 %copy-start.6 = (s32[4,2]{1,0:T(4,128)S(1)}, s32[4,2]{1,0:T(4,128)}, u32[]{:S(2)}) copy-start(s32[4,2]{1,0:T(4,128)} %broadcast_subtract_fusion.places) | copy-start | bytes 100
  21.1 26.1 %all-to-all-start = ((f32[32,4,3,128]{3,1,2,0:T(4,128)}), f32[32,4,3,128]{3,1,2,0:T(4,128)S(1)}, u32[]{:S(2)}, u32[]{:S(2)}) async-start(f32[32,4,3,128]{3,1,2,0:T(4,128)} %copy.37), calls=%async_computation | async-start | bytes 393216 | tf_op jit(solution)/shard_map/all_to_all | solution.py:323
  36.1 6.9 %collective-permute-start.2 = (f32[2,4,64,128]{3,2,1,0:T(8,128)}, f32[2,4,64,128]{3,2,1,0:T(8,128)S(1)}, u32[]{:S(2)}, u32[]{:S(2)}) collective-permute-start(f32[2,4,64,128]{3,2,1,0:T(8,128)} %get-tuple-element.19), channel_id=1, source_target_pairs={{0,1},{1,2},{2,3},{3,4},{4,5},{5,6},{6,7},{8,9},{9,10},{10,11},{11... | collective-permute-start | bytes 786440 | tf_op jit(solution)/shard_map/ppermute | solution.py:20
  38.3 4.8 %collective-permute-start.3 = (f32[2,4,64,128]{3,2,1,0:T(8,128)}, f32[2,4,64,128]{3,2,1,0:T(8,128)S(1)}, u32[]{:S(2)}, u32[]{:S(2)}) collective-permute-start(f32[2,4,64,128]{3,2,1,0:T(8,128)} %get-tuple-element.20), channel_id=1, source_target_pairs={{1,0},{2,1},{3,2},{4,3},{5,4},{6,5},{7,6},{9,8},{10,9},{11,10},{12... | collective-permute-start | bytes 786440 | tf_op jit(solution)/shard_map/ppermute | solution.py:20
  43.0 0.7 copy-start.4
  43.1 0.7 copy-start.5
  47.2 17.1 %all-to-all-start.1 = ((f32[4,32,1024]{2,1,0:T(8,128)}), f32[4,32,1024]{2,1,0:T(8,128)S(1)}, u32[]{:S(2)}, u32[]{:S(2)}) async-start(f32[4,32,1024]{2,1,0:T(8,128)} %bitcast.22), calls=%async_computation.1 | async-start | bytes 1048576 | tf_op jit(solution)/shard_map/all_to_all | solution.py:321
  64.3 10.4 %copy-start = (f32[4,32,1024]{2,1,0:T(8,128)}, f32[4,32,1024]{2,1,0:T(8,128)S(1)}, u32[]{:S(2)}) copy-start(f32[4,32,1024]{2,1,0:T(8,128)S(1)} %all-to-all-done.1.sino_ref) | copy-start | bytes 1572868
  65.0 17.9 %all-to-all-start.2 = ((f32[32,4,2,128]{3,1,2,0:T(4,128)}), f32[32,4,2,128]{3,1,2,0:T(4,128)S(1)}, u32[]{:S(2)}, u32[]{:S(2)}) async-start(f32[32,4,2,128]{3,1,2,0:T(4,128)} %broadcast_in_dim.43), calls=%async_computation.2 | async-start | bytes 262144 | tf_op jit(solution)/shard_map/all_to_all | solution.py:328
  74.7 8.2 %copy-start.1 = (f32[2,128,128]{2,1,0:T(8,128)S(1)}, f32[2,128,128]{2,1,0:T(8,128)}, u32[]{:S(2)}) copy-start(f32[2,128,128]{2,1,0:T(8,128)} %probe_ref.3) | copy-start | bytes 393220

commit v4 on v3

--- a/solution.py
+++ b/solution.py
@@ -78,9 +78,9 @@
     half = (up_ref.shape[0] - ROWS) // 2
     lane = lax.broadcasted_iota(jnp.int32, (ROWS, width), 1)
     note = jnp.zeros((ROWS, width), jnp.int32)
-    for b in range(places.shape[0]):
+    for b in range(places.shape[1]):
         for i in range(2):
-            note = jnp.where(lane == 2 * b + i, places[b, i] + 1, note)
+            note = jnp.where(lane == 2 * b + i, places[i, b] + 1, note)
     note = note.astype(jnp.float32)
     for ch in range(2):
         up_ref[ch * half:(ch + 1) * half] = block_ref[ch, :half]
@@ -184,9 +184,10 @@
             up_ref[ch, b] = column[ch, :half]
             add_columns(own_ref, (ch, slice(None)), column[ch, half:half + band], base, shift)
             down_ref[ch, b] = column[ch, half + band:]
-    stat_ref[:, 0, :] = numer_real
-    stat_ref[:, 1, :] = numer_imag
-    stat_ref[:, 2, :] = denom
+    share = stat_ref.shape[2]
+    for ch, value in enumerate((numer_real, numer_imag, denom)):
+        for i in range(stat_ref.shape[0]):
+            stat_ref[i, ch] = value[i * share:(i + 1) * share]
 
 
 def update_kernel(near, object_ref, own_ref, weight_ref, above_ref, below_ref, out_ref, imag_ref, total):
@@ -254,6 +255,7 @@
     vmem = pl.BlockSpec(memory_space=pltpu.VMEM)
     smem = pl.BlockSpec(memory_space=pltpu.SMEM)
     layer = object_field[0]
+    shares = lax.axis_size("angle") * lax.axis_size("pos")
     count = offsets.shape[1]
     packed = jax.ShapeDtypeStruct((2 * half + ROWS, width), f32)
     to_above, to_below = pl.pallas_call(
@@ -262,7 +264,7 @@
         out_shape=(packed, packed),
         in_specs=[smem, vmem],
         out_specs=[vmem] * 2,
-    )(offsets[0], layer)
+    )(offsets[0].T, layer)
     low = passed_along(to_below, "pos", 1)
     high = passed_along(to_above, "pos", -1)
     anchor = lax.axis_index("pos") * band - half
@@ -290,7 +292,7 @@
             jax.ShapeDtypeStruct((2, count, half, patch), f32),
             jax.ShapeDtypeStruct((2, band, width), f32),
             jax.ShapeDtypeStruct((2, count, half, patch), f32),
-            jax.ShapeDtypeStruct((patch, 3, patch), f32),
+            jax.ShapeDtypeStruct((shares, 3, patch // shares, patch), f32),
         ),
         in_specs=[smem] + [vmem] * 6 + [pl.BlockSpec(memory_space=pl.ANY)],
         out_specs=[vmem] * 4,
@@ -316,17 +318,14 @@
         scratch_shapes=[pltpu.VMEM((2, band, width), f32)],
     )(near, layer, own, weight, from_above, from_below)
     everyone = ("angle", "pos")
-    shares = lax.axis_size("angle") * lax.axis_size("pos")
     angles = lax.axis_size("angle")
     regrouped = lax.all_to_all(imag.reshape(angles, band // angles, width), "angle", split_axis=0, concat_axis=0, tiled=True)
-    pieces = stats.reshape(shares, patch // shares, 3, patch)
-    shared = lax.all_to_all(pieces, everyone, split_axis=0, concat_axis=0, tiled=True)
+    shared = lax.all_to_all(stats, everyone, split_axis=0, concat_axis=0, tiled=True)
     mine = jnp.sum(shared, axis=0)
-    step = mine[:, :2] / (mine[:, 2:] + 1.0)
+    step = mine[:2] / (mine[2:] + 1.0)
     copies = jnp.broadcast_to(step[None], (shares,) + step.shape)
-    copies, regrouped = lax.optimization_barrier((copies, regrouped))
     steps = lax.all_to_all(copies, everyone, split_axis=0, concat_axis=0, tiled=True)
-    new_probe = probe_field + jnp.swapaxes(steps.reshape(patch, 2, patch), 0, 1)
+    new_probe = probe_field + jnp.swapaxes(steps, 0, 1).reshape(2, patch, patch)
     rows = band // angles
     zwin = interp_index.shape[1]
     columns = min(BINS, width)

time: 84.1 us -> 81 us (0.963)
  starting transfers between devices: 36.6 us -> 28.9 us
  waiting for transfers between devices: 13.1 us -> 20.1 us
  local copies, waits for them, and re-layouts: 5.45 us -> 4 us
    all_to_all x1, starting transfers between devices: 9.68 us -> 2.78 us  [on_device(): lax.all_to_all(copies, everyone, split_axis=0, concat_axis=0, tiled=True)]
    all_to_all x1, waiting for transfers between devices: 0.01 us -> 5.16 us  [on_device(): lax.all_to_all(stats, everyone, split_axis=0, concat_axis=0, tiled=True)]
    all_to_all x1, waiting for transfers between devices: 12.2 us -> 14.1 us  [on_device(): lax.all_to_all(imag.reshape(angles, band // angles, width), 'angle', spli...]
    reshape x1 -> x0, local copies, waits for them, and re-layouts: 1.68 us -> none  [on_device(): pieces = stats.reshape(shares, patch // shares, 3, patch)]
    unnamed x14, local copies, waits for them, and re-layouts: 1.51 us -> 2.37 us
  transfers between devices with their start and end apart: 7 -> 7, of which waited for: 3 -> 3; matrix products, arithmetic and copies ran while one was open for 3% -> 5% of each run, Pallas kernels for 20% -> 11%
where the time goes in v4:
time: 81 us; the launch traced here: 80.5 us
  starting transfers between devices  28.9 us (36%)
  Pallas kernels  24.2 us (30%)
  waiting for transfers between devices  20.1 us (25%)
  local copies, waits for them, and re-layouts  4 us (5%)
  other arithmetic  2.51 us (3%)
    all_to_all x1, starting transfers between devices, on_device(): lax.all_to_all(stats, everyone, split_axis=0, concat_axis=0, tiled=True)  15 us
    all_to_all x1, waiting for transfers between devices, on_device(): lax.all_to_all(imag.reshape(angles, band // angles, width), 'angle', spli...  14.1 us
    pallas_call x1, Pallas kernels, on_device(): pl.pallas_call(back_kernel, name='back', grid=(width // columns,), out_sh...  7.31 us
    ppermute x4, starting transfers between devices, passed_along(): return lax.ppermute(array, axis, pairs)  7.17 us
    pallas_call x1, Pallas kernels, on_device(): pl.pallas_call(gradient_kernel, name='gradient', out_shape=(jax.ShapeDtyp...  5.44 us
    all_to_all x1, waiting for transfers between devices, on_device(): lax.all_to_all(stats, everyone, split_axis=0, concat_axis=0, tiled=True)  5.16 us
    all_to_all x1, starting transfers between devices, on_device(): lax.all_to_all(imag.reshape(angles, band // angles, width), 'angle', spli...  3.99 us
    pallas_call x1, Pallas kernels, on_device(): pl.pallas_call(update_kernel, name='update', out_shape=(jax.ShapeDtypeStr...  3.42 us
  transfers between devices with their start and end apart: 7, of which 3 were waited for; matrix products, arithmetic and copies ran while one was open for 5% of the time, Pallas kernels for 11%

profile of v4, /device:TPU:0, one launch (start us, length us, event | category | flops | bytes accessed | tf_op | source)
XLA Modules:
  0.0 80.5 jit_solution(16602121015484495802)
XLA Ops:
  0.6 2.3 %pack.1 = (f32[136,1024]{1,0:T(8,128)}, f32[136,1024]{1,0:T(8,128)}) custom-call(s32[2,4]{1,0:T(2,128)} %bitcast.23, f32[2,128,1024]{2,1,0:T(8,128)} %bitcast.15), custom_call_target="tpu_custom_call" | custom-call | tf_op jit(solution)/shard_map/pack/pallas_call | solution.py:261
  2.9 2.4 %collective-permute-start = (f32[136,1024]{1,0:T(8,128)}, f32[136,1024]{1,0:T(8,128)S(1)}, u32[]{:S(2)}, u32[]{:S(2)}) collective-permute-start(f32[136,1024]{1,0:T(8,128)} %get-tuple-element.13), channel_id=1, source_target_pairs={{0,1},{1,2},{2,3},{3,4},{4,5},{5,6},{6,7},{8,9},{9,10},{10,11},{11... | collective-permute-start | bytes 1671176 | tf_op jit(solution)/shard_map/ppermute | solution.py:20
  5.3 1.3 %collective-permute-start.1 = (f32[136,1024]{1,0:T(8,128)}, f32[136,1024]{1,0:T(8,128)S(1)}, u32[]{:S(2)}, u32[]{:S(2)}) collective-permute-start(f32[136,1024]{1,0:T(8,128)} %get-tuple-element.14), channel_id=1, source_target_pairs={{1,0},{2,1},{3,2},{4,3},{5,4},{6,5},{7,6},{9,8},{10,9},{11,10},{12... | collective-permute-start | bytes 1671176 | tf_op jit(solution)/shard_map/ppermute | solution.py:20
  6.6 0.8 copy.25
  7.4 3.4 %ramp.1 = (bf16[1024,1024]{1,0:T(8,128)(2,1)}, bf16[1024,1024]{1,0:T(8,128)(2,1)}) custom-call(), custom_call_target="tpu_custom_call" | custom-call | flops 20971520 | bytes 4194304 | tf_op jit(solution)/shard_map/ramp/pallas_call | solution.py:280
  10.8 0.1 pad_add_fusion.2
  10.9 0.1 pad_add_fusion
  11.0 0.5 broadcast_subtract_fusion.places
  11.5 0.0 collective-permute-done.low_ref
  11.5 0.0 copy-start.2
  11.5 0.1 convert_element_type.19
  11.6 0.0 collective-permute-done.1.high_ref
  11.6 0.0 copy-start.3
  11.7 0.1 convert_element_type.22
  11.7 0.6 copy-done.2
  12.4 0.1 copy-done.3
  12.5 0.0 copy-start.6
  12.5 5.4 %gradient.1 = (f32[2,4,64,128]{3,2,1,0:T(8,128)}, f32[2,128,1024]{2,1,0:T(8,128)}, f32[2,4,64,128]{3,2,1,0:T(8,128)}, f32[32,3,4,128]{3,2,1,0:T(4,128)}) custom-call(s32[4,2]{1,0:T(4,128)} %broadcast_subtract_fusion.places, f32[136,1024]{1,0:T(8,128)} %copy-done.2, f32[2,128,1024]{2,1,0:T(8,128)} %bitcast.16, f32[136,1024]{1,0:T(8,128)} %copy-done.3, ...), custom_call_target="tpu_custom_call" | custom-call | tf_op jit(solution)/shard_map/gradient/pallas_call | solution.py:288
  18.0 15.0 %all-to-all-start = ((f32[32,3,4,128]{3,2,1,0:T(4,128)}), f32[32,3,4,128]{3,2,1,0:T(4,128)S(1)}, u32[]{:S(2)}, u32[]{:S(2)}) async-start(f32[32,3,4,128]{3,2,1,0:T(4,128)} %get-tuple-element.20), calls=%async_computation | async-start | bytes 393216 | tf_op jit(solution)/shard_map/all_to_all | solution.py:323
  32.9 0.2 fusion.4
  33.2 2.2 %collective-permute-start.2 = (f32[2,4,64,128]{3,2,1,0:T(8,128)}, f32[2,4,64,128]{3,2,1,0:T(8,128)S(1)}, u32[]{:S(2)}, u32[]{:S(2)}) collective-permute-start(f32[2,4,64,128]{3,2,1,0:T(8,128)} %get-tuple-element.17), channel_id=1, source_target_pairs={{0,1},{1,2},{2,3},{3,4},{4,5},{5,6},{6,7},{8,9},{9,10},{10,11},{11... | collective-permute-start | bytes 786440 | tf_op jit(solution)/shard_map/ppermute | solution.py:20
  35.4 1.3 %collective-permute-start.3 = (f32[2,4,64,128]{3,2,1,0:T(8,128)}, f32[2,4,64,128]{3,2,1,0:T(8,128)S(1)}, u32[]{:S(2)}, u32[]{:S(2)}) collective-permute-start(f32[2,4,64,128]{3,2,1,0:T(8,128)} %get-tuple-element.18), channel_id=1, source_target_pairs={{1,0},{2,1},{3,2},{4,3},{5,4},{6,5},{7,6},{9,8},{10,9},{11,10},{12... | collective-permute-start | bytes 786440 | tf_op jit(solution)/shard_map/ppermute | solution.py:20
  36.7 0.1 subtract_select_fusion
  36.7 5.2 %all-to-all-done = f32[32,3,4,128]{3,2,1,0:T(4,128)S(1)} async-done(((f32[32,3,4,128]{3,2,1,0:T(4,128)}), f32[32,3,4,128]{3,2,1,0:T(4,128)S(1)}, u32[]{:S(2)}, u32[]{:S(2)}) %all-to-all-start) | async-done | bytes 196640 | tf_op jit(solution)/shard_map/all_to_all | solution.py:323
  41.9 0.1 reduce_sum.9
  42.0 0.7 broadcast_in_dim.43
  42.6 2.8 %all-to-all-start.1 = ((f32[32,2,4,128]{3,2,1,0:T(4,128)}), f32[32,2,4,128]{3,2,1,0:T(4,128)S(1)}, u32[]{:S(2)}, u32[]{:S(2)}) async-start(f32[32,2,4,128]{3,2,1,0:T(4,128)} %broadcast_in_dim.43), calls=%async_computation.1 | async-start | bytes 262144 | tf_op jit(solution)/shard_map/all_to_all | solution.py:327
  45.4 0.1 subtract_select_fusion.1
  45.5 0.0 copy-done.6
  45.5 0.7 fusion.near
  46.2 2.3 %weight.1.weight_ref = f32[128,1024]{1,0:T(8,128)} custom-call(s32[12,3]{1,0:T(8,128)} %fusion.near, f32[2,128,128]{2,1,0:T(8,128)} %probe_ref.3), custom_call_target="tpu_custom_call" | custom-call | flops 20971520 | bytes 524288 | tf_op jit(solution)/shard_map/weight/pallas_call | solution.py:303
  48.5 0.0 collective-permute-done.2.above_ref
  48.5 0.0 copy-start.4
  48.5 0.0 collective-permute-done.3.below_ref
  48.5 0.0 copy-start.5
  48.5 0.7 copy-done.4
  49.2 0.1 copy-done.5
  49.3 0.0 copy-start.1
  49.3 3.4 %update.1 = (f32[2,128,1024]{2,1,0:T(8,128)}, f32[128,1024]{1,0:T(8,128)}) custom-call(s32[12,3]{1,0:T(8,128)} %fusion.near, f32[2,128,1024]{2,1,0:T(8,128)} %bitcast.17, f32[2,128,1024]{2,1,0:T(8,128)} %get-tuple-element.16.own_ref, f32[128,1024]{1,0:T(8,128)} %weight.1.weight_ref, f32[2,4,64,128]{3,2,1,0:T(8,128)} %copy-done.4, f32[2,4,64,128]{3,2,1,0:T(8,128)} %copy-done.5), custom_call_target="tpu_custom_call" | custom-call | tf_op jit(solution)/shard_map/update/pallas_call | solution.py:312
  52.7 0.9 %all-to-all-done.1 = f32[32,2,4,128]{3,2,1,0:T(4,128)S(1)} async-done(((f32[32,2,4,128]{3,2,1,0:T(4,128)}), f32[32,2,4,128]{3,2,1,0:T(4,128)S(1)}, u32[]{:S(2)}, u32[]{:S(2)}) %all-to-all-start.1) | async-done | bytes 131104 | tf_op jit(solution)/shard_map/all_to_all | solution.py:327
  53.6 4.0 %all-to-all-start.2 = ((f32[4,32,1024]{2,1,0:T(8,128)}), f32[4,32,1024]{2,1,0:T(8,128)S(1)}, u32[]{:S(2)}, u32[]{:S(2)}) async-start(f32[4,32,1024]{2,1,0:T(8,128)} %bitcast.19), calls=%async_computation.2 | async-start | bytes 1048576 | tf_op jit(solution)/shard_map/all_to_all | solution.py:322
  57.6 0.0 copy-done.1
  57.7 0.7 add.25
  58.3 14.1 %all-to-all-done.2.sino_ref = f32[4,32,1024]{2,1,0:T(8,128)S(1)} async-done(((f32[4,32,1024]{2,1,0:T(8,128)}), f32[4,32,1024]{2,1,0:T(8,128)S(1)}, u32[]{:S(2)}, u32[]{:S(2)}) %all-to-all-start.2) | async-done | bytes 524320 | tf_op jit(solution)/shard_map/all_to_all | solution.py:322
  72.4 0.0 copy-start
  72.4 0.8 %copy-done = f32[4,32,1024]{2,1,0:T(8,128)} copy-done((f32[4,32,1024]{2,1,0:T(8,128)}, f32[4,32,1024]{2,1,0:T(8,128)S(1)}, u32[]{:S(2)}) %copy-start) | copy-done | bytes 524312
  73.2 7.3 %back.1 = f32[32,2,1024]{2,1,0:T(2,128)} custom-call(f32[4,32,1024]{2,1,0:T(8,128)} %copy-done, bf16[1024,1024]{1,0:T(8,128)(2,1)} %get-tuple-element.15.ramp_ref.ramp_high_ref, bf16[1024,1024]{1,0:T(8,128)(2,1)} %get-tuple-element.22.ramp_low_ref, s32[4,2,1024]{2,1,0:T(2,128)} %index_ref.1, f32[4,2,1024]{2,1,0:T(2,128)} %weight_ref.1), custom_call_target="tpu_custom_call" | custom-call | tf_op jit(solution)/shard_map/back/pallas_call | solution.py:332
  (7 shorter events, 0.1 us)
Async XLA Ops:
  2.9 8.6 %collective-permute-start = (f32[136,1024]{1,0:T(8,128)}, f32[136,1024]{1,0:T(8,128)S(1)}, u32[]{:S(2)}, u32[]{:S(2)}) collective-permute-start(f32[136,1024]{1,0:T(8,128)} %get-tuple-element.13), channel_id=1, source_target_pairs={{0,1},{1,2},{2,3},{3,4},{4,5},{5,6},{6,7},{8,9},{9,10},{10,11},{11... | collective-permute-start | bytes 1671176 | tf_op jit(solution)/shard_map/ppermute | solution.py:20
  5.3 6.3 %collective-permute-start.1 = (f32[136,1024]{1,0:T(8,128)}, f32[136,1024]{1,0:T(8,128)S(1)}, u32[]{:S(2)}, u32[]{:S(2)}) collective-permute-start(f32[136,1024]{1,0:T(8,128)} %get-tuple-element.14), channel_id=1, source_target_pairs={{1,0},{2,1},{3,2},{4,3},{5,4},{6,5},{7,6},{9,8},{10,9},{11,10},{12... | collective-permute-start | bytes 1671176 | tf_op jit(solution)/shard_map/ppermute | solution.py:20
  11.5 0.8 %copy-start.2 = (f32[136,1024]{1,0:T(8,128)}, f32[136,1024]{1,0:T(8,128)S(1)}, u32[]{:S(2)}) copy-start(f32[136,1024]{1,0:T(8,128)S(1)} %collective-permute-done.low_ref) | copy-start | bytes 1671172
  11.6 0.9 %copy-start.3 = (f32[136,1024]{1,0:T(8,128)}, f32[136,1024]{1,0:T(8,128)S(1)}, u32[]{:S(2)}) copy-start(f32[136,1024]{1,0:T(8,128)S(1)} %collective-permute-done.1.high_ref) | copy-start | bytes 1671172
  12.5 33.0 %copy-start.6 = (s32[4,2]{1,0:T(4,128)S(1)}, s32[4,2]{1,0:T(4,128)}, u32[]{:S(2)}) copy-start(s32[4,2]{1,0:T(4,128)} %broadcast_subtract_fusion.places) | copy-start | bytes 100
  18.0 23.9 %all-to-all-start = ((f32[32,3,4,128]{3,2,1,0:T(4,128)}), f32[32,3,4,128]{3,2,1,0:T(4,128)S(1)}, u32[]{:S(2)}, u32[]{:S(2)}) async-start(f32[32,3,4,128]{3,2,1,0:T(4,128)} %get-tuple-element.20), calls=%async_computation | async-start | bytes 393216 | tf_op jit(solution)/shard_map/all_to_all | solution.py:323
  33.2 15.3 %collective-permute-start.2 = (f32[2,4,64,128]{3,2,1,0:T(8,128)}, f32[2,4,64,128]{3,2,1,0:T(8,128)S(1)}, u32[]{:S(2)}, u32[]{:S(2)}) collective-permute-start(f32[2,4,64,128]{3,2,1,0:T(8,128)} %get-tuple-element.17), channel_id=1, source_target_pairs={{0,1},{1,2},{2,3},{3,4},{4,5},{5,6},{6,7},{8,9},{9,10},{10,11},{11... | collective-permute-start | bytes 786440 | tf_op jit(solution)/shard_map/ppermute | solution.py:20
  35.4 13.2 %collective-permute-start.3 = (f32[2,4,64,128]{3,2,1,0:T(8,128)}, f32[2,4,64,128]{3,2,1,0:T(8,128)S(1)}, u32[]{:S(2)}, u32[]{:S(2)}) collective-permute-start(f32[2,4,64,128]{3,2,1,0:T(8,128)} %get-tuple-element.18), channel_id=1, source_target_pairs={{1,0},{2,1},{3,2},{4,3},{5,4},{6,5},{7,6},{9,8},{10,9},{11,10},{12... | collective-permute-start | bytes 786440 | tf_op jit(solution)/shard_map/ppermute | solution.py:20
  42.6 11.0 %all-to-all-start.1 = ((f32[32,2,4,128]{3,2,1,0:T(4,128)}), f32[32,2,4,128]{3,2,1,0:T(4,128)S(1)}, u32[]{:S(2)}, u32[]{:S(2)}) async-start(f32[32,2,4,128]{3,2,1,0:T(4,128)} %broadcast_in_dim.43), calls=%async_computation.1 | async-start | bytes 262144 | tf_op jit(solution)/shard_map/all_to_all | solution.py:327
  48.5 0.7 copy-start.4
  48.5 0.8 copy-start.5
  49.3 8.3 %copy-start.1 = (f32[2,128,128]{2,1,0:T(8,128)S(1)}, f32[2,128,128]{2,1,0:T(8,128)}, u32[]{:S(2)}) copy-start(f32[2,128,128]{2,1,0:T(8,128)} %probe_ref.3) | copy-start | bytes 393220
  53.6 18.8 %all-to-all-start.2 = ((f32[4,32,1024]{2,1,0:T(8,128)}), f32[4,32,1024]{2,1,0:T(8,128)S(1)}, u32[]{:S(2)}, u32[]{:S(2)}) async-start(f32[4,32,1024]{2,1,0:T(8,128)} %bitcast.19), calls=%async_computation.2 | async-start | bytes 1048576 | tf_op jit(solution)/shard_map/all_to_all | solution.py:322
  72.4 0.8 %copy-start = (f32[4,32,1024]{2,1,0:T(8,128)}, f32[4,32,1024]{2,1,0:T(8,128)S(1)}, u32[]{:S(2)}) copy-start(f32[4,32,1024]{2,1,0:T(8,128)S(1)} %all-to-all-done.2.sino_ref) | copy-start | bytes 1572868
